TPU v7x, 1024 devices: a whole 4x8x16 slice. The times are simulated.
1024 devices in a mesh: sfc: 128 (over z, y), sub: 8 (over x, core).
Axes of the slice: x: 4, y: 8, z: 16, core: 2. Of those that a mesh axis runs over, the one named last changes fastest.
Arguments:
- vectors: float32 [64, 16384, 256], P(None, ('sfc', 'sub')), may hold values from -10 to 10
- reaction: float32 [16384, 256], P(('sfc', 'sub')), may hold values from 0.5 to 5
Outputs:
- basis: float32 [64, 16384, 256], P(None, ('sfc', 'sub'))
- upper: float32 [64, 64], replicated
All inputs are finite; a program needn't handle non-finite values.
Results may differ from a plain program's by a relative error of at most 0.0003.
Values sent between devices are 32-bit elements; how exact they have to be, the bound alone decides.
No kernel may reach another device: no remote copies, remote signals or barrier semaphores. Data moves between devices by JAX's collectives and lax.ppermute only.
A program may use at most 32 MiB of HBM per device.

v0:
```python
import functools
import math

import jax
import jax.numpy as jnp
from jax import lax
from jax.sharding import Mesh
from jax.sharding import PartitionSpec as P

NY = 32
NL = 8
POWERS = 3
SFC_SUB = ("sfc_0", "sfc_1", "sub_0", "sub_1")
SFC = ("sfc_0", "sfc_1")
SUB = ("sub_0", "sub_1")


DELTA_MASS = 0.5


def extended(shard, sides, width):
    edges = {}
    for axis, dim in sides:
        peers, length = (lax.axis_size(axis), shard.shape[dim])
        up = [(i, (i + 1) % peers) for i in range(peers - 1)]
        last = lax.slice_in_dim(shard, length - width, length, axis=dim)
        leading = lax.slice_in_dim(shard, 0, width, axis=dim)
        edges[dim] = (
            lax.ppermute(last, axis, up),
            lax.ppermute(leading, axis, [(b, a) for a, b in up]),
        )
    done = []
    for _, dim in sides:
        low, high = edges[dim]
        around = [(width, width) if d in done else (0, 0) for d in range(shard.ndim)]
        shard = jnp.concatenate([jnp.pad(low, around), shard, jnp.pad(high, around)], axis=dim)
        done.append(dim)
    return shard


def over_axes(shard, axes):
    return functools.reduce(lax.psum, axes, shard)


def line_tables(count):
    index = jnp.arange(count)
    offset = index[:, None] - index[None, :]
    near = (jnp.abs(offset) == 1).astype(jnp.float32)
    same = (offset == 0).astype(jnp.float32)
    mass = (4.0 * same + near) / 6.0
    stiff = 2.0 * same - near
    return (mass, stiff)


def tables(across, layers):
    mass_across, stiff_across = line_tables(across)
    mass_layers, stiff_layers = line_tables(layers)
    mass_plane = jnp.kron(mass_layers, mass_across)
    stiff_plane = (
        jnp.kron(mass_layers, stiff_across)
        + jnp.kron(stiff_layers, mass_across)
        + DELTA_MASS * mass_plane
    )
    return jnp.concatenate([mass_plane, stiff_plane], axis=1)


def plane_products(field, table):
    plane = table.shape[0]
    both = jnp.einsum("kzp,pq->kzq", field, table, precision=lax.Precision.HIGHEST)
    return (both[..., :plane], both[..., plane:])


def operate(field, reaction, table):
    massed, mixed = plane_products(field, table)
    edge_term = mixed / 6.0 - massed
    padded = extended(edge_term, ((SFC_SUB, 1),), 1)
    neighbours = padded[:, :-2] + padded[:, 2:]
    return neighbours + 4.0 / 6.0 * mixed + 2.0 * massed + reaction[None] * field


def whole_factor(local):
    gram = jnp.dot(local, local.T, precision=lax.Precision.HIGHEST)
    total = over_axes(gram, SFC_SUB)
    return jnp.linalg.cholesky(total)


def lower_solve(lower, block):
    return lax.linalg.triangular_solve(lower, block, left_side=True, lower=True)


def per_device(vectors, reaction):
    table = tables(NY, NL)
    field = vectors
    for _ in range(POWERS):
        field = operate(field, reaction, table)
    local = field.reshape(field.shape[0], -1)
    lower_one = whole_factor(local)
    first = lower_solve(lower_one, local)
    lower_two = whole_factor(first)
    second = lower_solve(lower_two, first)
    scale = math.sqrt(lax.axis_size(SFC) * lax.axis_size(SUB) * local.shape[1])
    upper = jnp.dot(lower_one, lower_two, precision=lax.Precision.HIGHEST).T / scale
    return ((second * scale).reshape(vectors.shape), upper)


def solution(mesh):
    torus = Mesh(mesh.devices.reshape(16, 8, 4, 2), ("sfc_0", "sfc_1", "sub_0", "sub_1"))
    in_specs = (P(None, SFC_SUB, None), P(SFC_SUB, None))
    out_specs = (P(None, SFC_SUB, None), P())
    return jax.shard_map(
        per_device, mesh=torus, in_specs=in_specs, out_specs=out_specs, check_vma=False
    )
```

profile of v0, /device:TPU:1, one launch (start us, length us, event | category | flops | bytes accessed | tf_op | source)
XLA Modules:
  0.0 293.4 jit_solution(2754341464599987795)
XLA Ops:
  2.2 2.3 convolution_bitcast_fusion
  4.7 4.5 %collective-permute-start = (f32[64,1,256]{2,0,1:T(8,128)S(1)}, f32[64,1,256]{2,0,1:T(8,128)S(1)}, u32[]{:S(2)}, u32[]{:S(2)}) collective-permute-start(f32[64,1,256]{2,0,1:T(8,128)S(1)} %get-tuple-element.8), channel_id=1, source_target_pairs={{0,1},{1,2},{2,3},{3,4},{4,5},{5,6},{6,7},{7,8},{8,9},{9,10},{10,1... | collective-permute-start | bytes 196616 | tf_op jit(solution)/shard_map/ppermute | solution.py:29
  9.2 12.8 %collective-permute-start.1 = (f32[64,1,256]{2,0,1:T(8,128)S(1)}, f32[64,1,256]{2,0,1:T(8,128)S(1)}, u32[]{:S(2)}, u32[]{:S(2)}) collective-permute-start(f32[64,1,256]{2,0,1:T(8,128)S(1)} %get-tuple-element.9), channel_id=1, source_target_pairs={{1,0},{2,1},{3,2},{4,3},{5,4},{6,5},{7,6},{8,7},{9,8},{10,9},{11,1... | collective-permute-start | bytes 196616 | tf_op jit(solution)/shard_map/ppermute | solution.py:30
  23.7 1.8 fusion.14
  25.8 1.9 collective-permute-start.2
  27.7 2.4 collective-permute-start.3
  30.1 3.2 %collective-permute-done.3 = f32[64,1,256]{2,0,1:T(8,128)S(1)} collective-permute-done((f32[64,1,256]{2,0,1:T(8,128)S(1)}, f32[64,1,256]{2,0,1:T(8,128)S(1)}, u32[]{:S(2)}, u32[]{:S(2)}) %collective-permute-start.3) | collective-permute-done | bytes 65568 | tf_op jit(solution)/shard_map/ppermute | solution.py:30
  33.6 1.8 fusion.13
  35.6 1.9 collective-permute-start.4
  37.6 2.4 collective-permute-start.5
  40.0 3.2 %collective-permute-done.5 = f32[64,1,256]{2,0,1:T(8,128)S(1)} collective-permute-done((f32[64,1,256]{2,0,1:T(8,128)S(1)}, f32[64,1,256]{2,0,1:T(8,128)S(1)}, u32[]{:S(2)}, u32[]{:S(2)}) %collective-permute-start.5) | collective-permute-done | bytes 65568 | tf_op jit(solution)/shard_map/ppermute | solution.py:30
  44.4 51.2 %psum.56 = f32[64,64]{0,1:T(8,128)S(1)} all-reduce(f32[64,64]{0,1:T(8,128)S(1)} %convolution_bitcast_fusion.1), channel_id=1, replica_groups=mesh['sfc_0'=16,'sfc_1'=8,'sub_0'=4,'sub_1'=2] {'sfc_0'}, use_global_device_ids=true, to_apply=%region_0.1 | all-reduce | flops 4096 | bytes 32768 | tf_op jit(solution)/shard_map/psum | solution.py:42
  95.6 20.1 %psum.57 = f32[64,64]{0,1:T(8,128)S(1)} all-reduce(f32[64,64]{0,1:T(8,128)S(1)} %psum.56), channel_id=1, replica_groups=mesh['sfc_0'=16,'sfc_1'=8,'sub_0'=4,'sub_1'=2] {'sfc_1'}, use_global_device_ids=true, to_apply=%region_1.2 | all-reduce | flops 4096 | bytes 32768 | tf_op jit(solution)/shard_map/psum | solution.py:42
  115.7 24.8 %psum.58 = f32[64,64]{0,1:T(8,128)S(1)} all-reduce(f32[64,64]{0,1:T(8,128)S(1)} %psum.57), channel_id=1, replica_groups=mesh['sfc_0'=16,'sfc_1'=8,'sub_0'=4,'sub_1'=2] {'sub_0'}, use_global_device_ids=true, to_apply=%region_2.3 | all-reduce | flops 4096 | bytes 32768 | tf_op jit(solution)/shard_map/psum | solution.py:42
  140.5 21.2 %psum.59 = f32[64,64]{0,1:T(8,128)S(1)} all-reduce(f32[64,64]{0,1:T(8,128)S(1)} %psum.58), channel_id=1, replica_groups=mesh['sfc_0'=16,'sfc_1'=8,'sub_0'=4,'sub_1'=2] {'sub_1'}, use_global_device_ids=true, to_apply=%region_3.4 | all-reduce | flops 4096 | bytes 32768 | tf_op jit(solution)/shard_map/psum | solution.py:42
  161.8 5.8 %cholesky.44 = f32[64,64]{1,0:T(8,128)S(1)} custom-call(f32[64,64]{1,0:T(8,128)S(1)} %fusion.19), custom_call_target="Cholesky" | custom-call | tf_op jit(solution)/shard_map/jit(cholesky)/cholesky | solution.py:84
  169.0 4.9 %custom-call.6 = f32[1,64,64]{1,2,0:T(8,128)S(1)} custom-call(f32[1,64,64]{2,1,0:T(8,128)S(1)} %fusion.23), custom_call_target="InvertDiagBlocksLowerTriangular" | custom-call | tf_op jit(solution)/shard_map/triangular_solve/custom-call.0 | solution.py:88
  176.0 39.8 %psum.60 = f32[64,64]{0,1:T(8,128)S(1)} all-reduce(f32[64,64]{0,1:T(8,128)S(1)} %fusion.44), channel_id=1, replica_groups=mesh['sfc_0'=16,'sfc_1'=8,'sub_0'=4,'sub_1'=2] {'sfc_0'}, use_global_device_ids=true, to_apply=%region_6.9 | all-reduce | flops 4096 | bytes 32768 | tf_op jit(solution)/shard_map/psum | solution.py:42
  215.8 20.8 %psum.61 = f32[64,64]{0,1:T(8,128)S(1)} all-reduce(f32[64,64]{0,1:T(8,128)S(1)} %psum.60), channel_id=1, replica_groups=mesh['sfc_0'=16,'sfc_1'=8,'sub_0'=4,'sub_1'=2] {'sfc_1'}, use_global_device_ids=true, to_apply=%region_7.10 | all-reduce | flops 4096 | bytes 32768 | tf_op jit(solution)/shard_map/psum | solution.py:42
  236.6 12.4 %psum.62 = f32[64,64]{0,1:T(8,128)S(1)} all-reduce(f32[64,64]{0,1:T(8,128)S(1)} %psum.61), channel_id=1, replica_groups=mesh['sfc_0'=16,'sfc_1'=8,'sub_0'=4,'sub_1'=2] {'sub_0'}, use_global_device_ids=true, to_apply=%region_8.11 | all-reduce | flops 4096 | bytes 32768 | tf_op jit(solution)/shard_map/psum | solution.py:42
  249.1 27.5 %psum.63 = f32[64,64]{0,1:T(8,128)S(1)} all-reduce(f32[64,64]{0,1:T(8,128)S(1)} %psum.62), channel_id=1, replica_groups=mesh['sfc_0'=16,'sfc_1'=8,'sub_0'=4,'sub_1'=2] {'sub_1'}, use_global_device_ids=true, to_apply=%region_9.12 | all-reduce | flops 4096 | bytes 32768 | tf_op jit(solution)/shard_map/psum | solution.py:42
  276.7 5.8 %cholesky.55 = f32[64,64]{1,0:T(8,128)S(1)} custom-call(f32[64,64]{1,0:T(8,128)S(1)} %fusion.16), custom_call_target="Cholesky" | custom-call | tf_op jit(solution)/shard_map/jit(cholesky)/cholesky | solution.py:84
  283.3 2.2 convolution_multiply_fusion.1
  286.2 4.9 %custom-call.7 = f32[1,64,64]{1,2,0:T(8,128)S(1)} custom-call(f32[1,64,64]{2,1,0:T(8,128)S(1)} %select_bitcast_fusion), custom_call_target="InvertDiagBlocksLowerTriangular" | custom-call | tf_op jit(solution)/shard_map/triangular_solve/custom-call.0 | solution.py:88
  (39 shorter events, 12.7 us)
Async XLA Ops:
  1.0 1.2 copy-start
  4.5 18.4 %copy-start.1 = (f32[16,256]{1,0:T(8,128)S(1)}, f32[16,256]{1,0:T(8,128)}, u32[]{:S(2)}) copy-start(f32[16,256]{1,0:T(8,128)} %param.6) | copy-start | bytes 49156
  4.7 17.3 %collective-permute-start = (f32[64,1,256]{2,0,1:T(8,128)S(1)}, f32[64,1,256]{2,0,1:T(8,128)S(1)}, u32[]{:S(2)}, u32[]{:S(2)}) collective-permute-start(f32[64,1,256]{2,0,1:T(8,128)S(1)} %get-tuple-element.8), channel_id=1, source_target_pairs={{0,1},{1,2},{2,3},{3,4},{4,5},{5,6},{6,7},{7,8},{8,9},{9,10},{10,1... | collective-permute-start | bytes 196616 | tf_op jit(solution)/shard_map/ppermute | solution.py:29
  9.2 13.7 %collective-permute-start.1 = (f32[64,1,256]{2,0,1:T(8,128)S(1)}, f32[64,1,256]{2,0,1:T(8,128)S(1)}, u32[]{:S(2)}, u32[]{:S(2)}) collective-permute-start(f32[64,1,256]{2,0,1:T(8,128)S(1)} %get-tuple-element.9), channel_id=1, source_target_pairs={{1,0},{2,1},{3,2},{4,3},{5,4},{6,5},{7,6},{8,7},{9,8},{10,9},{11,1... | collective-permute-start | bytes 196616 | tf_op jit(solution)/shard_map/ppermute | solution.py:30
  25.8 4.3 %collective-permute-start.2 = (f32[64,1,256]{2,0,1:T(8,128)S(1)}, f32[64,1,256]{2,0,1:T(8,128)S(1)}, u32[]{:S(2)}, u32[]{:S(2)}) collective-permute-start(f32[64,1,256]{2,0,1:T(8,128)S(1)} %get-tuple-element.6), channel_id=1, source_target_pairs={{0,1},{1,2},{2,3},{3,4},{4,5},{5,6},{6,7},{7,8},{8,9},{9,10},{10,1... | collective-permute-start | bytes 196616 | tf_op jit(solution)/shard_map/ppermute | solution.py:29
  27.7 5.6 %collective-permute-start.3 = (f32[64,1,256]{2,0,1:T(8,128)S(1)}, f32[64,1,256]{2,0,1:T(8,128)S(1)}, u32[]{:S(2)}, u32[]{:S(2)}) collective-permute-start(f32[64,1,256]{2,0,1:T(8,128)S(1)} %get-tuple-element.7), channel_id=1, source_target_pairs={{1,0},{2,1},{3,2},{4,3},{5,4},{6,5},{7,6},{8,7},{9,8},{10,9},{11,1... | collective-permute-start | bytes 196616 | tf_op jit(solution)/shard_map/ppermute | solution.py:30
  35.6 4.3 %collective-permute-start.4 = (f32[64,1,256]{2,0,1:T(8,128)S(1)}, f32[64,1,256]{2,0,1:T(8,128)S(1)}, u32[]{:S(2)}, u32[]{:S(2)}) collective-permute-start(f32[64,1,256]{2,0,1:T(8,128)S(1)} %get-tuple-element.4), channel_id=1, source_target_pairs={{0,1},{1,2},{2,3},{3,4},{4,5},{5,6},{6,7},{7,8},{8,9},{9,10},{10,1... | collective-permute-start | bytes 196616 | tf_op jit(solution)/shard_map/ppermute | solution.py:29
  37.6 5.6 %collective-permute-start.5 = (f32[64,1,256]{2,0,1:T(8,128)S(1)}, f32[64,1,256]{2,0,1:T(8,128)S(1)}, u32[]{:S(2)}, u32[]{:S(2)}) collective-permute-start(f32[64,1,256]{2,0,1:T(8,128)S(1)} %get-tuple-element.5), channel_id=1, source_target_pairs={{1,0},{2,1},{3,2},{4,3},{5,4},{6,5},{7,6},{8,7},{9,8},{10,9},{11,1... | collective-permute-start | bytes 196616 | tf_op jit(solution)/shard_map/ppermute | solution.py:30
where the time goes:
time: 294 us; the launch traced here: 293 us
  blocking collectives  218 us (74%)
  other arithmetic  26.6 us (9%)
  starting transfers between devices  26 us (9%)
  matrix products  12.2 us (4%)
  waiting for transfers between devices  7.2 us (2%)
    psum x8, blocking collectives, over_axes(): return functools.reduce(lax.psum, axes, shard)  218 us
    ppermute x3, starting transfers between devices, extended(): lax.ppermute(leading, axis, [(b, a) for a, b in up])  17.6 us
    another operation x6, other arithmetic, whole_factor(): return jnp.linalg.cholesky(total)  13.1 us
    another operation x4, other arithmetic, lower_solve(): return lax.linalg.triangular_solve(lower, block, left_side=True, lower=True)  11.1 us
    ppermute x3, starting transfers between devices, extended(): lax.ppermute(last, axis, up)  8.34 us
    ppermute x3, waiting for transfers between devices, extended(): lax.ppermute(leading, axis, [(b, a) for a, b in up])  7.19 us
    dot_general x3, matrix products, plane_products(): jnp.einsum('kzp,pq->kzq', field, table, precision=lax.Precision.HIGHEST)  5.98 us
  transfers between devices with their start and end apart: 6, of which 3 were waited for; matrix products, arithmetic and copies ran while one was open for 0% of the time, Pallas kernels for 0%

commit v1 on v0

v1 whole, which is shorter than its diff:
```python
import math

import jax
import jax.numpy as jnp
from jax import lax
from jax.experimental import pallas as pl
from jax.experimental.pallas import tpu as pltpu
from jax.sharding import Mesh
from jax.sharding import PartitionSpec as P

NY = 32
NL = 8
PLANE = NY * NL
POWERS = 3
SFC_SUB = ("sfc_0", "sfc_1", "sub_0", "sub_1")
FAR = ("sfc_0",)
NEAR = ("sfc_1", "sub_0", "sub_1")
DELTA_MASS = 0.5
F32 = jnp.float32
BF16 = jnp.bfloat16
HIGHEST = lax.Precision.HIGHEST


def line_tables(count):
    index = jnp.arange(count)
    offset = index[:, None] - index[None, :]
    near = (jnp.abs(offset) == 1).astype(F32)
    same = (offset == 0).astype(F32)
    return 4.0 * same + near, 2.0 * same - near


def tables():
    mass_across, stiff_across = line_tables(NY)
    mass_layers, stiff_layers = line_tables(NL)
    mass = jnp.kron(mass_layers, mass_across)
    stiff = (
        6.0 * (jnp.kron(mass_layers, stiff_across) + jnp.kron(stiff_layers, mass_across))
        + DELTA_MASS * mass
    )
    return jnp.concatenate([stiff - 6.0 * mass, 4.0 * stiff + 12.0 * mass], axis=1).astype(BF16)


def split3(value):
    one = value.astype(BF16)
    rest = value - one.astype(F32)
    two = rest.astype(BF16)
    three = (rest - two.astype(F32)).astype(BF16)
    return one, two, three


def dot(a, b):
    return lax.dot_general(a, b, (((1,), (0,)), ((), ())), preferred_element_type=F32)


def dot_t(a, b):
    return lax.dot_general(a, b, (((1,), (1,)), ((), ())), preferred_element_type=F32)


def two_sum(a, b):
    s = a + b
    t = s - a
    return s, (a - (s - t)) + (b - t)


def power_below(x, square=False):
    low = -60 if square else -120
    p = jnp.full_like(x, 2.0**low)
    q = jnp.full_like(x, 2.0**-low)
    for k in (64, 32, 16, 8, 4, 2, 1) if square else (128, 64, 32, 16, 8, 4, 2, 1):
        half = 2.0 ** (k // 2) if k > 1 else 2.0
        up = p * half * (half if k > 1 else 1.0)
        down = q * (1.0 / half) * (1.0 / half if k > 1 else 1.0)
        fits = (up * up if square else up) <= x
        p, q = jnp.where(fits, up, p), jnp.where(fits, down, q)
    return p, q


def digits(value, count, extra=None, extra_at=3):
    out = []
    rest = value
    for i in range(count):
        digit = jnp.round(rest)
        out.append(digit.astype(BF16))
        rest = rest - digit
        if extra is not None and i == extra_at - 1:
            rest = rest + extra * (256.0 ** (extra_at - 1))
        rest = rest * 256.0
    return out


def levels_to_pair(levels):
    high = levels[-1]
    low = jnp.zeros_like(high)
    for level in reversed(levels[:-1]):
        high, err = two_sum(level, high * (1.0 / 256.0))
        low = low * (1.0 / 256.0) + err
    return high, low


def operator_kernel(k, nx, vec_ref, react_ref, low_ref, high_ref, inside_ref, table_ref, w_ref, gram_ref, field, react, both):
    halo = POWERS
    total = nx + 2 * halo
    for x in range(nx):
        field[halo + x] = vec_ref[:, x, :]
    for x in range(halo):
        field[x] = low_ref[:k, x, :]
        field[halo + nx + x] = high_ref[:k, x, :]
    react[0:halo] = low_ref[k]
    react[halo : halo + nx] = react_ref[...]
    react[halo + nx : total] = high_ref[k]
    low_inside = inside_ref[0]
    high_inside = inside_ref[1]
    table = table_ref[...]
    for step in range(POWERS):
        first, last = step, total - step

        def product(x, _):
            rows = field[x]
            one, two, three = split3(rows)
            both[x] = dot(one, table) + dot(two, table) + dot(three, table)
            return 0

        lax.fori_loop(first, last, product, 0)

        def combine(x, _):
            value = (
                both[x - 1, :, :PLANE] + both[x + 1, :, :PLANE] + both[x, :, PLANE:]
            ) * (1.0 / 216.0) + react[pl.ds(x, 1), :] * field[x]
            keep = jnp.where(x < halo, low_inside, jnp.where(x >= halo + nx, high_inside, 1.0))
            field[x] = value * keep
            return 0

        lax.fori_loop(first + 1, last - 1, combine, 0)
    peak = jnp.abs(field[halo])
    for x in range(1, nx):
        peak = jnp.maximum(peak, jnp.abs(field[halo + x]))
    peak = jnp.max(peak, axis=1, keepdims=True)
    size, inverse = power_below(peak)
    scale = inverse * 64.0
    slices = 4
    group = 4
    pairs = None
    for start in range(0, nx, group):
        parts = [[] for _ in range(slices)]
        for x in range(start, start + group):
            for s, digit in enumerate(digits(field[halo + x] * scale, slices)):
                parts[s].append(digit)
        stack = jnp.concatenate([jnp.concatenate(p, axis=1) for p in parts], axis=0)
        counts = dot_t(stack, stack)
        block = [[counts[i * k : (i + 1) * k, j * k : (j + 1) * k] for j in range(slices)] for i in range(slices)]
        tail = [
            sum(block[i][level - i] for i in range(slices) if 0 <= level - i < slices)
            for level in range(3, 2 * slices - 1)
        ]
        rest = tail[-1]
        for value in reversed(tail[:-1]):
            rest = value + rest * (1.0 / 256.0)
        terms = [
            rest * 2.0**-24,
            block[1][1] * 2.0**-16,
            (block[0][2] + block[2][0]) * 2.0**-16,
            block[0][1] * 2.0**-8,
            block[1][0] * 2.0**-8,
            block[0][0],
        ]
        for term in terms:
            if pairs is None:
                pairs = (term, jnp.zeros_like(term))
            else:
                high, err = two_sum(pairs[0], term)
                pairs = (high, pairs[1] + err)
    high, err = two_sum(pairs[0], pairs[1])
    row = size * (1.0 / 64.0)
    eye = lax.broadcasted_iota(jnp.int32, (k, k), 0) == lax.broadcasted_iota(jnp.int32, (k, k), 1)
    column = jnp.sum(jnp.where(eye, row, 0.0), axis=0, keepdims=True)
    gram_ref[:, 0, :] = jnp.concatenate([high * row * column, err * row * column], axis=1)
    for x in range(nx):
        w_ref[x] = field[halo + x]


def operator_and_gram(vectors, reaction, low, high, inside):
    k, nx, plane = vectors.shape
    total = nx + 2 * POWERS
    vmem = pl.BlockSpec(memory_space=pltpu.VMEM)
    smem = pl.BlockSpec(memory_space=pltpu.SMEM)
    return pl.pallas_call(
        lambda *refs: operator_kernel(k, nx, *refs),
        out_shape=(
            jax.ShapeDtypeStruct((nx, k, plane), F32),
            jax.ShapeDtypeStruct((k, 1, 2 * k), F32),
        ),
        in_specs=[vmem, vmem, vmem, vmem, smem, vmem],
        out_specs=(vmem, vmem),
        scratch_shapes=[
            pltpu.VMEM((total, k, plane), F32),
            pltpu.VMEM((total, plane), F32),
            pltpu.VMEM((total, k, 2 * plane), F32),
        ],
        name="operator_gram",
    )(vectors, reaction, low, high, inside, tables())


def pair_sum_kernel(parts_ref, out_ref):
    value = parts_ref[:, 0, :]
    width = value.shape[1]
    half = width // 2
    error = jnp.zeros_like(value)
    while value.shape[0] > 1:
        n = value.shape[0] // 2
        value, err = two_sum(value[:n], value[n:])
        error = error[:n] + error[n:] + err
    low = pltpu.roll(value, half, 1) + error
    high, err = two_sum(value, low)
    lane = lax.broadcasted_iota(jnp.int32, value.shape, 1)
    row = jnp.where(lane < half, high, pltpu.roll(err, half, 1))
    out_ref[:, 0, :] = jnp.broadcast_to(row, (out_ref.shape[0], width))


def pair_sum(parts, copies):
    return pl.pallas_call(
        pair_sum_kernel,
        out_shape=jax.ShapeDtypeStruct((copies, 1, parts.shape[2]), F32),
        in_specs=[pl.BlockSpec(memory_space=pltpu.VMEM)],
        out_specs=pl.BlockSpec(memory_space=pltpu.VMEM),
        name="pair_sum",
    )(parts)


def sum_over_devices(gram):
    near = lax.axis_size(NEAR)
    far = lax.axis_size(FAR)
    rows = lax.all_to_all(gram, NEAR, 0, 0)
    mine = pair_sum(rows, far)
    mine = pair_sum(lax.all_to_all(mine, FAR, 0, 0), near)
    return lax.all_to_all(mine, NEAR, 0, 0)


def level_sums(counts, k, rows, columns):
    out = []
    for level in range(rows + columns - 1):
        terms = [
            counts[i * k : (i + 1) * k, (level - i) * k : (level - i + 1) * k]
            for i in range(rows)
            if 0 <= level - i < columns
        ]
        total = terms[0]
        for term in terms[1:]:
            total = total + term
        out.append(total)
    return out


def whiten_kernel(gram_ref, guess_ref, gram_two_ref, exact_ref, product_ref):
    k = gram_ref.shape[0]
    pair = gram_ref[:, 0, :]
    high, low = pair[:, :k], pair[:, k:]
    eye = lax.broadcasted_iota(jnp.int32, (k, k), 0) == lax.broadcasted_iota(jnp.int32, (k, k), 1)
    diagonal = jnp.where(eye, high, 0.0)
    size_row, inverse_row = power_below(jnp.sum(diagonal, axis=0, keepdims=True), square=True)
    _, inverse_column = power_below(jnp.sum(diagonal, axis=1, keepdims=True), square=True)
    scale = inverse_column * inverse_row
    gram_digits = digits(high * scale * 32.0, 6, extra=low * scale * 32.0)
    guess = guess_ref[...] * size_row
    top, top_inverse = power_below(jnp.max(jnp.abs(guess), axis=1, keepdims=True))
    guess_digits = digits(guess * top_inverse * 64.0, 3)
    exact = sum(d.astype(F32) * 256.0**-i for i, d in enumerate(guess_digits))
    exact_ref[...] = exact * (top * (1.0 / 64.0)) * inverse_row
    guess_stack = jnp.concatenate(guess_digits, axis=0)
    counts = dot(guess_stack, jnp.concatenate(gram_digits, axis=1))
    high, low = levels_to_pair(level_sums(counts, k, 3, 6))
    product_ref[...] = (high + low) * (top * 2.0**-11) * size_row
    big, big_inverse = power_below(jnp.max(jnp.abs(high), axis=1, keepdims=True))
    product_digits = digits(high * big_inverse * 64.0, 6, extra=low * big_inverse * 64.0)
    counts = dot_t(jnp.concatenate(product_digits, axis=0), guess_stack)
    high, low = levels_to_pair(level_sums(counts, k, 6, 3))
    top_row = jnp.sum(jnp.where(eye, top, 0.0), axis=0, keepdims=True)
    gram_two_ref[...] = (high + low) * (top * 2.0**-11) * (big * (1.0 / 64.0)) * (top_row * (1.0 / 64.0))


def whiten(gram, guess):
    k = guess.shape[0]
    vmem = pl.BlockSpec(memory_space=pltpu.VMEM)
    square = jax.ShapeDtypeStruct((k, k), F32)
    return pl.pallas_call(
        whiten_kernel,
        out_shape=(square, square, square),
        in_specs=[vmem, vmem],
        out_specs=(vmem, vmem, vmem),
        name="whiten",
    )(gram, guess)


def lower_inverse(lower):
    eye = jnp.eye(lower.shape[0], dtype=F32)
    return lax.linalg.triangular_solve(lower, eye, left_side=True, lower=True)


def basis_kernel(scale, w_ref, factor_ref, rest_ref, out_ref):
    high, low = two_sum(factor_ref[...] * scale, rest_ref[...] * scale)
    p1, p2, p3 = split3(high)
    p4 = low.astype(BF16)
    left = jnp.concatenate([p1, p1, p1, p2, p2, p3, p4], axis=1)
    for x in range(w_ref.shape[0]):
        w1, w2, w3 = split3(w_ref[x])
        right = jnp.concatenate([w3, w2, w1, w2, w1, w1, w1], axis=0)
        out_ref[:, x, :] = dot(left, right)


def basis_of(w, factor, rest, scale):
    nx, k, plane = w.shape
    vmem = pl.BlockSpec(memory_space=pltpu.VMEM)
    return pl.pallas_call(
        lambda *refs: basis_kernel(scale, *refs),
        out_shape=jax.ShapeDtypeStruct((k, nx, plane), F32),
        in_specs=[vmem, vmem, vmem],
        out_specs=vmem,
        name="basis",
    )(w, factor, rest)


def per_device(vectors, reaction):
    k, nx, plane = vectors.shape
    peers = lax.axis_size(SFC_SUB)
    me = lax.axis_index(SFC_SUB)
    up = [(i, i + 1) for i in range(peers - 1)]
    down = [(i + 1, i) for i in range(peers - 1)]
    last = jnp.concatenate([vectors[:, nx - POWERS :], reaction[None, nx - POWERS :]], axis=0)
    leading = jnp.concatenate([vectors[:, :POWERS], reaction[None, :POWERS]], axis=0)
    low = lax.ppermute(last, SFC_SUB, up)
    high = lax.ppermute(leading, SFC_SUB, down)
    inside = jnp.stack([me > 0, me < peers - 1]).astype(F32)
    w, gram = operator_and_gram(vectors, reaction, low, high, inside)
    gram = sum_over_devices(gram)
    guess = lower_inverse(jnp.linalg.cholesky(gram[:, 0, :k]))
    gram_two, exact, product = whiten(gram, guess)
    second = lower_inverse(jnp.linalg.cholesky(gram_two))
    eye = jnp.eye(k, dtype=F32)
    rest = jnp.dot(second - eye, exact, precision=HIGHEST)
    scale = math.sqrt(peers * nx * plane)
    upper = jnp.triu(jnp.dot(second, product, precision=HIGHEST)) / scale
    return basis_of(w, exact, rest, scale), upper


def solution(mesh):
    torus = Mesh(mesh.devices.reshape(16, 8, 4, 2), ("sfc_0", "sfc_1", "sub_0", "sub_1"))
    in_specs = (P(None, SFC_SUB, None), P(SFC_SUB, None))
    out_specs = (P(None, SFC_SUB, None), P())
    return jax.shard_map(
        per_device, mesh=torus, in_specs=in_specs, out_specs=out_specs, check_vma=False
    )
```

time: 294 us -> 143 us (0.49)
  blocking collectives: 218 us -> 43.1 us
  Pallas kernels: 0 us -> 30.3 us
  matrix products: 12.2 us -> 2.66 us
  local copies, waits for them, and re-layouts: 2.74 us -> 6.24 us
    psum x8 -> x0, blocking collectives: 218 us -> none  [over_axes(): return functools.reduce(lax.psum, axes, shard)]
    all_to_all x0 -> x2, blocking collectives: none -> 43.1 us  [the longest x1 29.4 us: sum_over_devices(): mine = pair_sum(lax.all_to_all(mine, FAR, 0, 0), near)]
    pallas_call x0 -> x5, Pallas kernels: none -> 30.3 us  [the longest x1 21.1 us: operator_and_gram(): pl.pallas_call(lambda *refs: operator_kernel(k, nx, *refs), out_shape=(ja...]
    all_to_all x0 -> x1, waiting for transfers between devices: none -> 9.43 us  [sum_over_devices(): return lax.all_to_all(mine, NEAR, 0, 0)]
    ppermute x6 -> x2, starting transfers between devices: 26 us -> 17.3 us  [the longest x1 12.8 us: per_device(): high = lax.ppermute(leading, SFC_SUB, down)]
    dot_general x6 -> x2, matrix products: 10.1 us -> 1.55 us  [the longest x1 0.78 us: per_device(): upper = jnp.triu(jnp.dot(second, product, precision=HIGHEST)) / scale]
    ppermute x6 -> x2, waiting for transfers between devices: 7.2 us -> 0.01 us  [the longest x1 0.01 us: per_device(): low = lax.ppermute(last, SFC_SUB, up)]
    all_to_all x0 -> x1, starting transfers between devices: none -> 6.08 us  [sum_over_devices(): return lax.all_to_all(mine, NEAR, 0, 0)]
  transfers between devices with their start and end apart: 6 -> 3, of which waited for: 3 -> 1; matrix products, arithmetic and copies ran while one was open for 0% -> 2% of each run, Pallas kernels for 0% -> 0%
where the time goes in v1:
time: 143 us; the launch traced here: 142 us
  blocking collectives  43.1 us (30%)
  Pallas kernels  30.3 us (21%)
  other arithmetic  26.2 us (18%)
  starting transfers between devices  23.4 us (16%)
  waiting for transfers between devices  9.43 us (7%)
  local copies, waits for them, and re-layouts  6.24 us (4%)
  matrix products  2.66 us (2%)
    all_to_all x1, blocking collectives, sum_over_devices(): mine = pair_sum(lax.all_to_all(mine, FAR, 0, 0), near)  29.4 us
    pallas_call x1, Pallas kernels, operator_and_gram(): pl.pallas_call(lambda *refs: operator_kernel(k, nx, *refs), out_shape=(ja...  21.1 us
    all_to_all x1, blocking collectives, sum_over_devices(): rows = lax.all_to_all(gram, NEAR, 0, 0)  13.7 us
    ppermute x1, starting transfers between devices, per_device(): high = lax.ppermute(leading, SFC_SUB, down)  12.8 us
    another operation x4, other arithmetic, lower_inverse(): return lax.linalg.triangular_solve(lower, eye, left_side=True, lower=True)  11.1 us
    all_to_all x1, waiting for transfers between devices, sum_over_devices(): return lax.all_to_all(mine, NEAR, 0, 0)  9.43 us
    another operation x3, other arithmetic, per_device(): guess = lower_inverse(jnp.linalg.cholesky(gram[:, 0, :k]))  6.53 us
    another operation x3, other arithmetic, per_device(): second = lower_inverse(jnp.linalg.cholesky(gram_two))  6.52 us
  transfers between devices with their start and end apart: 3, of which 1 were waited for; matrix products, arithmetic and copies ran while one was open for 2% of the time, Pallas kernels for 0%

profile of v1, /device:TPU:1, one launch (start us, length us, event | category | flops | bytes accessed | tf_op | source)
XLA Modules:
  0.0 142.2 jit_solution(13640763306422659788)
XLA Ops:
  0.6 0.7 slice_bitcast_fusion
  1.4 1.3 fusion.18
  2.7 4.5 %collective-permute-start = (f32[65,3,256]{2,1,0:T(4,128)S(1)}, f32[65,3,256]{2,1,0:T(4,128)S(1)}, u32[]{:S(2)}, u32[]{:S(2)}) collective-permute-start(f32[65,3,256]{2,1,0:T(4,128)S(1)} %pad_maximum_fusion), channel_id=1, source_target_pairs={{0,1},{1,2},{2,3},{3,4},{4,5},{5,6},{6,7},{7,8},{8,9},{9,10},{10,1... | collective-permute-start | bytes 599048 | tf_op jit(solution)/shard_map/ppermute | solution.py:329
  7.3 12.8 %collective-permute-start.1 = (f32[65,3,256]{2,1,0:T(4,128)S(1)}, f32[65,3,256]{2,1,0:T(4,128)S(1)}, u32[]{:S(2)}, u32[]{:S(2)}) collective-permute-start(f32[65,3,256]{2,1,0:T(4,128)S(1)} %pad_maximum_fusion.1), channel_id=1, source_target_pairs={{1,0},{2,1},{3,2},{4,3},{5,4},{6,5},{7,6},{8,7},{9,8},{10,9},{11,1... | collective-permute-start | bytes 599048 | tf_op jit(solution)/shard_map/ppermute | solution.py:330
  22.1 0.7 pad_maximum_fusion.2.refs_5_
  22.8 0.7 copy-done.1
  23.5 0.7 copy-done.2
  24.2 21.1 %operator_gram.1 = (f32[16,64,256]{2,1,0:T(8,128)}, f32[64,1,128]{2,1,0:T(1,128)}) custom-call(f32[64,16,256]{2,1,0:T(8,128)} %refs_0_.1, f32[16,256]{1,0:T(8,128)} %refs_1_.1, f32[65,3,256]{2,1,0:T(4,128)} %copy-done.1, f32[65,3,256]{2,1,0:T(4,128)} %copy-done.2, f32[2]{0:T(128)} %add_convert_fusion.refs_4_, bf16[256,512]{1,0:T(8,128)(2,1)} %pad_maximum_fusion.2.refs_5_), custom_call_target="tpu_custom_call" | custom-call | tf_op jit(solution)/shard_map/operator_gram/pallas_call | solution.py:186
  45.3 13.7 %all_to_all.15.parts_ref = f32[64,1,128]{2,1,0:T(1,128)} all-to-all(f32[64,1,128]{2,1,0:T(1,128)} %get-tuple-element.10), channel_id=1, replica_groups=mesh['sfc_0'=16,'sfc_1'=8,'sub_0'=4,'sub_1'=2] {'sfc_1','sub_0','sub_1'}, dimensions={0} | all-to-all | bytes 65536 | tf_op jit(solution)/shard_map/all_to_all | solution.py:232
  59.0 1.5 %pair_sum.2 = f32[16,1,128]{2,1,0:T(1,128)} custom-call(f32[64,1,128]{2,1,0:T(1,128)} %all_to_all.15.parts_ref), custom_call_target="tpu_custom_call" | custom-call | tf_op jit(solution)/shard_map/pair_sum/pallas_call | solution.py:220
  60.6 29.4 %all_to_all.16.parts_ref = f32[16,1,128]{2,1,0:T(1,128)} all-to-all(f32[16,1,128]{2,1,0:T(1,128)} %pair_sum.2), channel_id=1, replica_groups=mesh['sfc_0'=16,'sfc_1'=8,'sub_0'=4,'sub_1'=2] {'sfc_0'}, dimensions={0} | all-to-all | bytes 16384 | tf_op jit(solution)/shard_map/all_to_all | solution.py:234
  90.0 1.5 %pair_sum.3 = f32[64,1,128]{2,1,0:T(1,128)} custom-call(f32[16,1,128]{2,1,0:T(1,128)} %all_to_all.16.parts_ref), custom_call_target="tpu_custom_call" | custom-call | tf_op jit(solution)/shard_map/pair_sum/pallas_call | solution.py:220
  91.5 6.1 %all-to-all-start.2 = ((f32[64,1,128]{2,1,0:T(1,128)}), f32[64,1,128]{2,1,0:T(1,128)S(1)}, u32[]{:S(2)}, u32[]{:S(2)}) async-start(f32[64,1,128]{2,1,0:T(1,128)} %pair_sum.3), calls=%async_computation.2 | async-start | bytes 65536 | tf_op jit(solution)/shard_map/all_to_all | solution.py:235
  97.5 9.4 %all-to-all-done.2.gram_ref = f32[64,1,128]{2,1,0:T(1,128)S(1)} async-done(((f32[64,1,128]{2,1,0:T(1,128)}), f32[64,1,128]{2,1,0:T(1,128)S(1)}, u32[]{:S(2)}, u32[]{:S(2)}) %all-to-all-start.2) | async-done | bytes 32800 | tf_op jit(solution)/shard_map/all_to_all | solution.py:235
  107.7 5.9 %cholesky.44 = f32[64,64]{1,0:T(8,128)S(1)} custom-call(f32[64,64]{1,0:T(8,128)S(1)} %copy.5), custom_call_target="Cholesky" | custom-call | tf_op jit(solution)/shard_map/jit(cholesky)/cholesky | solution.py:334
  114.9 4.9 %custom-call.6 = f32[1,64,64]{1,2,0:T(8,128)S(1)} custom-call(f32[1,64,64]{2,1,0:T(8,128)S(1)} %fusion.10), custom_call_target="InvertDiagBlocksLowerTriangular" | custom-call | tf_op jit(solution)/shard_map/triangular_solve/custom-call.0 | solution.py:295
  119.8 0.9 fusion.8.guess_ref
  120.6 3.1 %whiten.1 = (f32[64,64]{1,0:T(8,128)}, f32[64,64]{1,0:T(8,128)}, f32[64,64]{1,0:T(8,128)}) custom-call(f32[64,1,128]{2,1,0:T(1,128)} %copy-done, f32[64,64]{1,0:T(8,128)} %fusion.8.guess_ref), custom_call_target="tpu_custom_call" | custom-call | tf_op jit(solution)/shard_map/whiten/pallas_call | solution.py:284
  123.7 0.9 copy.6
  124.7 5.8 %cholesky.55 = f32[64,64]{1,0:T(8,128)S(1)} custom-call(f32[64,64]{1,0:T(8,128)S(1)} %fusion.14), custom_call_target="Cholesky" | custom-call | tf_op jit(solution)/shard_map/jit(cholesky)/cholesky | solution.py:336
  131.9 4.9 %custom-call.7 = f32[1,64,64]{1,2,0:T(8,128)S(1)} custom-call(f32[1,64,64]{2,1,0:T(8,128)S(1)} %fusion.11), custom_call_target="InvertDiagBlocksLowerTriangular" | custom-call | tf_op jit(solution)/shard_map/triangular_solve/custom-call.0 | solution.py:295
  137.5 0.8 fusion.12.refs_2_
  138.3 0.8 fusion
  139.1 3.1 %basis.1 = f32[64,16,256]{2,1,0:T(8,128)} custom-call(f32[16,64,256]{2,1,0:T(8,128)} %get-tuple-element.9.refs_0_, f32[64,64]{1,0:T(8,128)} %get-tuple-element.11.refs_1_, f32[64,64]{1,0:T(8,128)} %fusion.12.refs_2_), custom_call_target="tpu_custom_call" | custom-call | tf_op jit(solution)/shard_map/basis/pallas_call | solution.py:312
  (32 shorter events, 6.2 us)
Async XLA Ops:
  2.7 20.1 %collective-permute-start = (f32[65,3,256]{2,1,0:T(4,128)S(1)}, f32[65,3,256]{2,1,0:T(4,128)S(1)}, u32[]{:S(2)}, u32[]{:S(2)}) collective-permute-start(f32[65,3,256]{2,1,0:T(4,128)S(1)} %pad_maximum_fusion), channel_id=1, source_target_pairs={{0,1},{1,2},{2,3},{3,4},{4,5},{5,6},{6,7},{7,8},{8,9},{9,10},{10,1... | collective-permute-start | bytes 599048 | tf_op jit(solution)/shard_map/ppermute | solution.py:329
  7.3 15.5 %collective-permute-start.1 = (f32[65,3,256]{2,1,0:T(4,128)S(1)}, f32[65,3,256]{2,1,0:T(4,128)S(1)}, u32[]{:S(2)}, u32[]{:S(2)}) collective-permute-start(f32[65,3,256]{2,1,0:T(4,128)S(1)} %pad_maximum_fusion.1), channel_id=1, source_target_pairs={{1,0},{2,1},{3,2},{4,3},{5,4},{6,5},{7,6},{8,7},{9,8},{10,9},{11,1... | collective-permute-start | bytes 599048 | tf_op jit(solution)/shard_map/ppermute | solution.py:330
  22.8 0.7 copy-start.1
  23.5 0.7 copy-start.2
  91.5 15.5 %all-to-all-start.2 = ((f32[64,1,128]{2,1,0:T(1,128)}), f32[64,1,128]{2,1,0:T(1,128)S(1)}, u32[]{:S(2)}, u32[]{:S(2)}) async-start(f32[64,1,128]{2,1,0:T(1,128)} %pair_sum.3), calls=%async_computation.2 | async-start | bytes 65536 | tf_op jit(solution)/shard_map/all_to_all | solution.py:235
  107.0 0.6 copy-start
  123.7 0.9 copy-start.4
  136.8 0.8 copy-start.3
  137.5 0.8 copy-start.5

commit v2 on v1

--- a/solution.py
+++ b/solution.py
@@ -2,6 +2,7 @@
 
 import jax
 import jax.numpy as jnp
+import numpy as np
 from jax import lax
 from jax.experimental import pallas as pl
 from jax.experimental.pallas import tpu as pltpu
@@ -22,22 +23,22 @@
 
 
 def line_tables(count):
-    index = jnp.arange(count)
+    index = np.arange(count)
     offset = index[:, None] - index[None, :]
-    near = (jnp.abs(offset) == 1).astype(F32)
-    same = (offset == 0).astype(F32)
+    near = (np.abs(offset) == 1).astype(np.float32)
+    same = (offset == 0).astype(np.float32)
     return 4.0 * same + near, 2.0 * same - near
 
 
 def tables():
     mass_across, stiff_across = line_tables(NY)
     mass_layers, stiff_layers = line_tables(NL)
-    mass = jnp.kron(mass_layers, mass_across)
+    mass = np.kron(mass_layers, mass_across)
     stiff = (
-        6.0 * (jnp.kron(mass_layers, stiff_across) + jnp.kron(stiff_layers, mass_across))
+        6.0 * (np.kron(mass_layers, stiff_across) + np.kron(stiff_layers, mass_across))
         + DELTA_MASS * mass
     )
-    return jnp.concatenate([stiff - 6.0 * mass, 4.0 * stiff + 12.0 * mass], axis=1).astype(BF16)
+    return np.concatenate([stiff - 6.0 * mass, 4.0 * stiff + 12.0 * mass], axis=1).astype(BF16)
 
 
 def split3(value):
@@ -100,40 +101,47 @@
 def operator_kernel(k, nx, vec_ref, react_ref, low_ref, high_ref, inside_ref, table_ref, w_ref, gram_ref, field, react, both):
     halo = POWERS
     total = nx + 2 * halo
+    chunk = 2
     for x in range(nx):
         field[halo + x] = vec_ref[:, x, :]
     for x in range(halo):
-        field[x] = low_ref[:k, x, :]
-        field[halo + nx + x] = high_ref[:k, x, :]
-    react[0:halo] = low_ref[k]
+        field[x] = low_ref[x, :k, :]
+        field[halo + nx + x] = high_ref[x, :k, :]
+    table = table_ref[...]
+    react[0:halo] = low_ref[:, k, :]
     react[halo : halo + nx] = react_ref[...]
-    react[halo + nx : total] = high_ref[k]
+    react[halo + nx : total] = high_ref[:, k, :]
     low_inside = inside_ref[0]
     high_inside = inside_ref[1]
-    table = table_ref[...]
     for step in range(POWERS):
         first, last = step, total - step
-
-        def product(x, _):
-            rows = field[x]
-            one, two, three = split3(rows)
-            both[x] = dot(one, table) + dot(two, table) + dot(three, table)
+        chunk = (22,20,18)[step]
+
+        def product(i, _):
+            x = first + chunk * i
+            one, two, three = split3(field[pl.ds(x, chunk)].reshape(chunk * k, PLANE))
+            parts = dot(jnp.concatenate([one, two, three], axis=0), table)
+            n = chunk * k
+            both[pl.ds(x, chunk)] = (parts[:n] + parts[n : 2 * n] + parts[2 * n :]).reshape(chunk, k, 2 * PLANE)
             return 0
 
-        lax.fori_loop(first, last, product, 0)
+        lax.fori_loop(0, (last - first) // chunk, product, 0)
 
         def combine(x, _):
             value = (
                 both[x - 1, :, :PLANE] + both[x + 1, :, :PLANE] + both[x, :, PLANE:]
             ) * (1.0 / 216.0) + react[pl.ds(x, 1), :] * field[x]
-            keep = jnp.where(x < halo, low_inside, jnp.where(x >= halo + nx, high_inside, 1.0))
-            field[x] = value * keep
+            if step < POWERS - 1:
+                keep = jnp.where(x < halo, low_inside, jnp.where(x >= halo + nx, high_inside, 1.0))
+                field[x] = value * keep
+            else:
+                w_ref[x - halo] = value
             return 0
 
-        lax.fori_loop(first + 1, last - 1, combine, 0)
-    peak = jnp.abs(field[halo])
+        lax.fori_loop(first + 1, last - 1, combine, 0, unroll=4)
+    peak = jnp.abs(w_ref[0])
     for x in range(1, nx):
-        peak = jnp.maximum(peak, jnp.abs(field[halo + x]))
+        peak = jnp.maximum(peak, jnp.abs(w_ref[x]))
     peak = jnp.max(peak, axis=1, keepdims=True)
     size, inverse = power_below(peak)
     scale = inverse * 64.0
@@ -143,7 +151,7 @@
     for start in range(0, nx, group):
         parts = [[] for _ in range(slices)]
         for x in range(start, start + group):
-            for s, digit in enumerate(digits(field[halo + x] * scale, slices)):
+            for s, digit in enumerate(digits(w_ref[x] * scale, slices)):
                 parts[s].append(digit)
         stack = jnp.concatenate([jnp.concatenate(p, axis=1) for p in parts], axis=0)
         counts = dot_t(stack, stack)
@@ -174,8 +182,6 @@
     eye = lax.broadcasted_iota(jnp.int32, (k, k), 0) == lax.broadcasted_iota(jnp.int32, (k, k), 1)
     column = jnp.sum(jnp.where(eye, row, 0.0), axis=0, keepdims=True)
     gram_ref[:, 0, :] = jnp.concatenate([high * row * column, err * row * column], axis=1)
-    for x in range(nx):
-        w_ref[x] = field[halo + x]
 
 
 def operator_and_gram(vectors, reaction, low, high, inside):
@@ -197,7 +203,7 @@
             pltpu.VMEM((total, k, 2 * plane), F32),
         ],
         name="operator_gram",
-    )(vectors, reaction, low, high, inside, tables())
+    )(vectors, reaction, low, high, inside, jnp.asarray(tables()))
 
 
 def pair_sum_kernel(parts_ref, out_ref):
@@ -250,55 +256,129 @@
     return out
 
 
-def whiten_kernel(gram_ref, guess_ref, gram_two_ref, exact_ref, product_ref):
+def dot_of_stack(a_parts, b_parts):
+    return dot(jnp.concatenate(a_parts, axis=1), jnp.concatenate(b_parts, axis=0))
+
+
+def dot_full(a, b):
+    a1, a2, a3 = split3(a)
+    b1, b2, b3 = split3(b)
+    return dot_of_stack([a1, a1, a2, a1, a2, a3], [b1, b2, b1, b3, b2, b1])
+
+
+def eliminate(square):
+    k = square.shape[0]
+    row = lax.broadcasted_iota(jnp.int32, (k, 2 * k), 0)
+    lane = lax.broadcasted_iota(jnp.int32, (k, 2 * k), 1)
+    eye = (row[:, :k] == lane[:, :k]).astype(F32)
+    block = 8
+    work = jnp.concatenate([square, eye], axis=1)
+    done = []
+    for start in range(0, k, block):
+        rows = work.shape[0]
+        columns = [jnp.broadcast_to(work[:, start + a : start + a + 1], (rows, 2 * k)) for a in range(block)]
+        below = lax.broadcasted_iota(jnp.int32, (rows, 2 * k), 0)
+        for a in range(block):
+            inverse = 1.0 / columns[a][a : a + 1, :]
+            many = jnp.where(below > a, columns[a] * inverse, 0.0)
+            for b in range(a + 1, block):
+                columns[b] = columns[b] - many * columns[b][a : a + 1, :]
+            work = work - many * work[a : a + 1, :]
+        done.append(work[:block])
+        work = work[block:]
+    work = jnp.concatenate(done, axis=0)
+    pivot = jnp.sum(work[:, :k] * eye, axis=1, keepdims=True)
+    return work[:, k:] * lax.rsqrt(pivot)
+
+
+def near_identity(delta, strict, half):
+    def lower(value):
+        return jnp.where(strict, value, jnp.where(half, 0.5 * value, 0.0))
+
+    y = -lower(delta)
+    for _ in range(3):
+        a = dot_full(y, delta)
+        outer = y + a
+        y1, y2, y3 = split3(y)
+        o1, o2, o3 = split3(outer)
+        square = dot_t(
+            jnp.concatenate([o1, o1, o2, o1, o2, o3], axis=1), jnp.concatenate([y1, y2, y1, y3, y2, y1], axis=1)
+        )
+        error = lower(delta + (y + y.T) + (a + a.T) + square)
+        y = y - error - dot_full(error, y)
+    return y
+
+
+def factor_kernel(scale, gram_ref, high_ref, low_ref, upper_ref, y_ref):
     k = gram_ref.shape[0]
     pair = gram_ref[:, 0, :]
     high, low = pair[:, :k], pair[:, k:]
-    eye = lax.broadcasted_iota(jnp.int32, (k, k), 0) == lax.broadcasted_iota(jnp.int32, (k, k), 1)
+    row = lax.broadcasted_iota(jnp.int32, (k, k), 0)
+    lane = lax.broadcasted_iota(jnp.int32, (k, k), 1)
+    eye = row == lane
     diagonal = jnp.where(eye, high, 0.0)
     size_row, inverse_row = power_below(jnp.sum(diagonal, axis=0, keepdims=True), square=True)
     _, inverse_column = power_below(jnp.sum(diagonal, axis=1, keepdims=True), square=True)
-    scale = inverse_column * inverse_row
-    gram_digits = digits(high * scale * 32.0, 6, extra=low * scale * 32.0)
-    guess = guess_ref[...] * size_row
+    unit = inverse_column * inverse_row
+    high = high * unit
+    low = low * unit
+    gram_digits = digits(high * 32.0, 6, extra=low * 32.0)
+    guess = eliminate(high)
     top, top_inverse = power_below(jnp.max(jnp.abs(guess), axis=1, keepdims=True))
     guess_digits = digits(guess * top_inverse * 64.0, 3)
     exact = sum(d.astype(F32) * 256.0**-i for i, d in enumerate(guess_digits))
-    exact_ref[...] = exact * (top * (1.0 / 64.0)) * inverse_row
+    exact = exact * (top * (1.0 / 64.0))
     guess_stack = jnp.concatenate(guess_digits, axis=0)
     counts = dot(guess_stack, jnp.concatenate(gram_digits, axis=1))
     high, low = levels_to_pair(level_sums(counts, k, 3, 6))
-    product_ref[...] = (high + low) * (top * 2.0**-11) * size_row
+    product = (high + low) * (top * 2.0**-11)
     big, big_inverse = power_below(jnp.max(jnp.abs(high), axis=1, keepdims=True))
     product_digits = digits(high * big_inverse * 64.0, 6, extra=low * big_inverse * 64.0)
     counts = dot_t(jnp.concatenate(product_digits, axis=0), guess_stack)
     high, low = levels_to_pair(level_sums(counts, k, 6, 3))
     top_row = jnp.sum(jnp.where(eye, top, 0.0), axis=0, keepdims=True)
-    gram_two_ref[...] = (high + low) * (top * 2.0**-11) * (big * (1.0 / 64.0)) * (top_row * (1.0 / 64.0))
-
-
-def whiten(gram, guess):
-    k = guess.shape[0]
+    unit = (top * 2.0**-11) * (big * (1.0 / 64.0)) * (top_row * (1.0 / 64.0))
+    high = high * unit
+    low = low * unit
+    delta = jnp.where(eye, high - 1.0, high) + low
+    worst = jnp.max(jnp.abs(delta))
+    small = worst < 2.0**-8
+
+    @pl.when(small)
+    def _():
+        y_ref[...] = near_identity(delta, row > lane, eye)
+
+    @pl.when(jnp.logical_not(small))
+    def _():
+        y_ref[...] = eliminate(high + low) - eye.astype(F32)
+
+    y = y_ref[...]
+    rest = dot_full(y, exact)
+    high, low = two_sum(exact, rest)
+    unit = inverse_row * scale
+    high_ref[...] = high * unit
+    low_ref[...] = low * unit
+    upper = product + dot_full(y, product)
+    upper_ref[...] = jnp.where(row <= lane, upper, 0.0) * (size_row * (1.0 / scale))
+
+
+def factor(gram, scale):
+    k = gram.shape[0]
     vmem = pl.BlockSpec(memory_space=pltpu.VMEM)
     square = jax.ShapeDtypeStruct((k, k), F32)
     return pl.pallas_call(
-        whiten_kernel,
+        lambda *refs: factor_kernel(scale, *refs),
         out_shape=(square, square, square),
-        in_specs=[vmem, vmem],
+        in_specs=[vmem],
         out_specs=(vmem, vmem, vmem),
-        name="whiten",
-    )(gram, guess)
-
-
-def lower_inverse(lower):
-    eye = jnp.eye(lower.shape[0], dtype=F32)
-    return lax.linalg.triangular_solve(lower, eye, left_side=True, lower=True)
-
-
-def basis_kernel(scale, w_ref, factor_ref, rest_ref, out_ref):
-    high, low = two_sum(factor_ref[...] * scale, rest_ref[...] * scale)
-    p1, p2, p3 = split3(high)
-    p4 = low.astype(BF16)
+        scratch_shapes=[pltpu.VMEM((k, k), F32)],
+        name="factor",
+    )(gram)
+
+
+def basis_kernel(w_ref, high_ref, low_ref, out_ref):
+    p1, p2, p3 = split3(high_ref[...])
+    p4 = low_ref[...].astype(BF16)
     left = jnp.concatenate([p1, p1, p1, p2, p2, p3, p4], axis=1)
     for x in range(w_ref.shape[0]):
         w1, w2, w3 = split3(w_ref[x])
@@ -306,16 +386,22 @@
         out_ref[:, x, :] = dot(left, right)
 
 
-def basis_of(w, factor, rest, scale):
+def basis_of(w, high, low):
     nx, k, plane = w.shape
     vmem = pl.BlockSpec(memory_space=pltpu.VMEM)
     return pl.pallas_call(
-        lambda *refs: basis_kernel(scale, *refs),
+        basis_kernel,
         out_shape=jax.ShapeDtypeStruct((k, nx, plane), F32),
         in_specs=[vmem, vmem, vmem],
         out_specs=vmem,
         name="basis",
-    )(w, factor, rest)
+    )(w, high, low)
+
+
+def border(vectors, reaction):
+    rows = jnp.swapaxes(vectors, 0, 1)
+    react = jnp.broadcast_to(reaction[:, None], (reaction.shape[0], 8, reaction.shape[1]))
+    return jnp.concatenate([rows, react], axis=1)
 
 
 def per_device(vectors, reaction):
@@ -324,21 +410,15 @@
     me = lax.axis_index(SFC_SUB)
     up = [(i, i + 1) for i in range(peers - 1)]
     down = [(i + 1, i) for i in range(peers - 1)]
-    last = jnp.concatenate([vectors[:, nx - POWERS :], reaction[None, nx - POWERS :]], axis=0)
-    leading = jnp.concatenate([vectors[:, :POWERS], reaction[None, :POWERS]], axis=0)
+    last = border(vectors[:, nx - POWERS :], reaction[nx - POWERS :])
+    leading = border(vectors[:, :POWERS], reaction[:POWERS])
     low = lax.ppermute(last, SFC_SUB, up)
     high = lax.ppermute(leading, SFC_SUB, down)
     inside = jnp.stack([me > 0, me < peers - 1]).astype(F32)
     w, gram = operator_and_gram(vectors, reaction, low, high, inside)
     gram = sum_over_devices(gram)
-    guess = lower_inverse(jnp.linalg.cholesky(gram[:, 0, :k]))
-    gram_two, exact, product = whiten(gram, guess)
-    second = lower_inverse(jnp.linalg.cholesky(gram_two))
-    eye = jnp.eye(k, dtype=F32)
-    rest = jnp.dot(second - eye, exact, precision=HIGHEST)
-    scale = math.sqrt(peers * nx * plane)
-    upper = jnp.triu(jnp.dot(second, product, precision=HIGHEST)) / scale
-    return basis_of(w, exact, rest, scale), upper
+    high, low, upper = factor(gram, math.sqrt(peers * nx * plane))
+    return basis_of(w, high, low), upper
 
 
 def solution(mesh):

time: 143 us -> 106 us (0.74)
  other arithmetic: 26.2 us -> 0.59 us
  blocking collectives: 43.1 us -> 60.9 us
  waiting for transfers between devices: 9.43 us -> 0.51 us
  Pallas kernels: 30.3 us -> 22 us
  starting transfers between devices: 23.4 us -> 17.3 us
  local copies, waits for them, and re-layouts: 6.24 us -> 2.96 us
  matrix products: 2.66 us -> 0 us
    another operation x11 -> x0, other arithmetic: 24.7 us -> none  [the longest x4 11.1 us: lower_inverse(): return lax.linalg.triangular_solve(lower, eye, left_side=True, lower=True)]
    all_to_all x0 -> x1, blocking collectives: none -> 16.1 us  [sum_over_devices(): return lax.all_to_all(mine, NEAR, 0, 0)]
    pallas_call x1, Pallas kernels: 21.1 us -> 8.33 us  [operator_and_gram(): pl.pallas_call(lambda *refs: operator_kernel(k, nx, *refs), out_shape=(ja...]
    all_to_all x1 -> x0, waiting for transfers between devices: 9.43 us -> none  [sum_over_devices(): return lax.all_to_all(mine, NEAR, 0, 0)]
    all_to_all x1 -> x0, starting transfers between devices: 6.08 us -> none  [sum_over_devices(): return lax.all_to_all(mine, NEAR, 0, 0)]
    pallas_call x2, Pallas kernels: 6.24 us -> 10.6 us  [the longest x1 7.49 us: factor(): pl.pallas_call(lambda *refs: factor_kernel(scale, *refs), out_shape=(squa...]
    dot_general x2 -> x0, matrix products: 1.55 us -> none  [the longest x1 0.78 us: per_device(): upper = jnp.triu(jnp.dot(second, product, precision=HIGHEST)) / scale]
    unnamed x12 -> x6, local copies, waits for them, and re-layouts: 2.48 us -> 0.94 us
  transfers between devices with their start and end apart: 3 -> 2, of which waited for: 1 -> 1; matrix products, arithmetic and copies ran while one was open for 2% -> 1% of each run, Pallas kernels for 0% -> 0%
where the time goes in v2:
time: 106 us; the launch traced here: 105 us
  blocking collectives  60.9 us (57%)
  Pallas kernels  22 us (21%)
  starting transfers between devices  17.3 us (16%)
  local copies, waits for them, and re-layouts  2.96 us (3%)
    all_to_all x1, blocking collectives, sum_over_devices(): mine = pair_sum(lax.all_to_all(mine, FAR, 0, 0), near)  29.8 us
    all_to_all x1, blocking collectives, sum_over_devices(): return lax.all_to_all(mine, NEAR, 0, 0)  16.1 us
    all_to_all x1, blocking collectives, sum_over_devices(): rows = lax.all_to_all(gram, NEAR, 0, 0)  15 us
    ppermute x1, starting transfers between devices, per_device(): high = lax.ppermute(leading, SFC_SUB, down)  12.8 us
    pallas_call x1, Pallas kernels, operator_and_gram(): pl.pallas_call(lambda *refs: operator_kernel(k, nx, *refs), out_shape=(ja...  8.33 us
    pallas_call x1, Pallas kernels, factor(): pl.pallas_call(lambda *refs: factor_kernel(scale, *refs), out_shape=(squa...  7.49 us
    ppermute x1, starting transfers between devices, per_device(): low = lax.ppermute(last, SFC_SUB, up)  4.5 us
    pallas_call x1, Pallas kernels, basis_of(): pl.pallas_call(basis_kernel, out_shape=jax.ShapeDtypeStruct((k, nx, plane...  3.13 us
  transfers between devices with their start and end apart: 2, of which 1 were waited for; matrix products, arithmetic and copies ran while one was open for 1% of the time, Pallas kernels for 0%

profile of v2, /device:TPU:1, one launch (start us, length us, event | category | flops | bytes accessed | tf_op | source)
XLA Modules:
  0.0 105.0 jit_solution(10398801246770428833)
XLA Ops:
  0.6 0.7 fusion.1
  1.4 1.3 %fusion = (f32[64,3,256]{2,1,0:T(4,128)S(1)}, f32[64,3,256]{2,1,0:T(4,128)S(1)}) fusion(f32[64,16,256]{2,1,0:T(8,128)} %refs_0_.1), kind=kLoop, calls=%fused_computation.5 | loop fusion | bytes 786432 | tf_op jit(solution)/shard_map/slice | solution.py:414
  2.7 4.5 %collective-permute-start = (f32[3,72,256]{2,1,0:T(8,128)S(1)}, f32[3,72,256]{2,1,0:T(8,128)S(1)}, u32[]{:S(2)}, u32[]{:S(2)}) collective-permute-start(f32[3,72,256]{2,1,0:T(8,128)S(1)} %pad_maximum_fusion), channel_id=1, source_target_pairs={{0,1},{1,2},{2,3},{3,4},{4,5},{5,6},{6,7},{7,8},{8,9},{9,10},{10,1... | collective-permute-start | bytes 663560 | tf_op jit(solution)/shard_map/ppermute | solution.py:415
  7.3 12.8 %collective-permute-start.1 = (f32[3,72,256]{2,1,0:T(8,128)S(1)}, f32[3,72,256]{2,1,0:T(8,128)S(1)}, u32[]{:S(2)}, u32[]{:S(2)}) collective-permute-start(f32[3,72,256]{2,1,0:T(8,128)S(1)} %pad_maximum_fusion.1), channel_id=1, source_target_pairs={{1,0},{2,1},{3,2},{4,3},{5,4},{6,5},{7,6},{8,7},{9,8},{10,9},{11,1... | collective-permute-start | bytes 663560 | tf_op jit(solution)/shard_map/ppermute | solution.py:416
  20.2 0.6 add_convert_fusion.refs_4_
  20.7 0.0 collective-permute-done.refs_2_
  20.7 0.0 copy-start
  20.7 0.5 collective-permute-done.1.refs_3_
  21.2 0.2 copy-done
  21.4 0.0 copy-start.1
  21.4 0.7 copy-done.1
  22.1 8.3 %operator_gram.1 = (f32[16,64,256]{2,1,0:T(8,128)}, f32[64,1,128]{2,1,0:T(1,128)}) custom-call(f32[64,16,256]{2,1,0:T(8,128)} %refs_0_.1, f32[16,256]{1,0:T(8,128)} %refs_1_.1, f32[3,72,256]{2,1,0:T(8,128)} %copy-done, f32[3,72,256]{2,1,0:T(8,128)} %copy-done.1, f32[2]{0:T(128)} %add_convert_fusion.refs_4_, bf16[256,512]{1,0:T(8,128)(2,1)} %constant.30.clone.refs_5_), custom_call_target="tpu_custom_call" | custom-call | tf_op jit(solution)/shard_map/operator_gram/pallas_call | solution.py:192
  30.4 15.0 %all_to_all.15.parts_ref = f32[64,1,128]{2,1,0:T(1,128)} all-to-all(f32[64,1,128]{2,1,0:T(1,128)} %get-tuple-element.8), channel_id=1, replica_groups=mesh['sfc_0'=16,'sfc_1'=8,'sub_0'=4,'sub_1'=2] {'sfc_1','sub_0','sub_1'}, dimensions={0} | all-to-all | bytes 65536 | tf_op jit(solution)/shard_map/all_to_all | solution.py:238
  45.4 1.5 %pair_sum.2 = f32[16,1,128]{2,1,0:T(1,128)} custom-call(f32[64,1,128]{2,1,0:T(1,128)} %all_to_all.15.parts_ref), custom_call_target="tpu_custom_call" | custom-call | tf_op jit(solution)/shard_map/pair_sum/pallas_call | solution.py:226
  47.0 29.8 %all_to_all.16.parts_ref = f32[16,1,128]{2,1,0:T(1,128)} all-to-all(f32[16,1,128]{2,1,0:T(1,128)} %pair_sum.2), channel_id=1, replica_groups=mesh['sfc_0'=16,'sfc_1'=8,'sub_0'=4,'sub_1'=2] {'sfc_0'}, dimensions={0} | all-to-all | bytes 16384 | tf_op jit(solution)/shard_map/all_to_all | solution.py:240
  76.7 1.5 %pair_sum.3 = f32[64,1,128]{2,1,0:T(1,128)} custom-call(f32[16,1,128]{2,1,0:T(1,128)} %all_to_all.16.parts_ref), custom_call_target="tpu_custom_call" | custom-call | tf_op jit(solution)/shard_map/pair_sum/pallas_call | solution.py:226
  78.2 16.1 %all_to_all.17.refs_0_ = f32[64,1,128]{2,1,0:T(1,128)} all-to-all(f32[64,1,128]{2,1,0:T(1,128)} %pair_sum.3), channel_id=1, replica_groups=mesh['sfc_0'=16,'sfc_1'=8,'sub_0'=4,'sub_1'=2] {'sfc_1','sub_0','sub_1'}, dimensions={0} | all-to-all | bytes 65536 | tf_op jit(solution)/shard_map/all_to_all | solution.py:241
  94.4 7.5 %factor.1 = (f32[64,64]{1,0:T(8,128)}, f32[64,64]{1,0:T(8,128)}, f32[64,64]{1,0:T(8,128)}) custom-call(f32[64,1,128]{2,1,0:T(1,128)} %all_to_all.17.refs_0_), custom_call_target="tpu_custom_call" | custom-call | tf_op jit(solution)/shard_map/factor/pallas_call | solution.py:369
  101.9 3.1 %basis.1 = f32[64,16,256]{2,1,0:T(8,128)} custom-call(f32[16,64,256]{2,1,0:T(8,128)} %get-tuple-element.7.w_ref, f32[64,64]{1,0:T(8,128)} %get-tuple-element.9.high_ref, f32[64,64]{1,0:T(8,128)} %get-tuple-element.10.low_ref), custom_call_target="tpu_custom_call" | custom-call | tf_op jit(solution)/shard_map/basis/pallas_call | solution.py:392
  (6 shorter events, 0.1 us)
Async XLA Ops:
  2.7 18.0 %collective-permute-start = (f32[3,72,256]{2,1,0:T(8,128)S(1)}, f32[3,72,256]{2,1,0:T(8,128)S(1)}, u32[]{:S(2)}, u32[]{:S(2)}) collective-permute-start(f32[3,72,256]{2,1,0:T(8,128)S(1)} %pad_maximum_fusion), channel_id=1, source_target_pairs={{0,1},{1,2},{2,3},{3,4},{4,5},{5,6},{6,7},{7,8},{8,9},{9,10},{10,1... | collective-permute-start | bytes 663560 | tf_op jit(solution)/shard_map/ppermute | solution.py:415
  7.3 13.9 %collective-permute-start.1 = (f32[3,72,256]{2,1,0:T(8,128)S(1)}, f32[3,72,256]{2,1,0:T(8,128)S(1)}, u32[]{:S(2)}, u32[]{:S(2)}) collective-permute-start(f32[3,72,256]{2,1,0:T(8,128)S(1)} %pad_maximum_fusion.1), channel_id=1, source_target_pairs={{1,0},{2,1},{3,2},{4,3},{5,4},{6,5},{7,6},{8,7},{9,8},{10,9},{11,1... | collective-permute-start | bytes 663560 | tf_op jit(solution)/shard_map/ppermute | solution.py:416
  20.7 0.7 copy-start
  21.4 0.7 copy-start.1

commit v3 on v2

--- a/solution.py
+++ b/solution.py
@@ -19,7 +19,18 @@
 DELTA_MASS = 0.5
 F32 = jnp.float32
 BF16 = jnp.bfloat16
-HIGHEST = lax.Precision.HIGHEST
+
+
+SMALL = pltpu.CompilerParams(vmem_limit_bytes=24 * 2**20)
+VMEM_SPEC = pl.BlockSpec(memory_space=pltpu.VMEM)
+
+
+def in_vmem(*shape):
+    return pltpu.VMEM(shape, F32)
+
+
+def vmem(array):
+    return pltpu.with_memory_space_constraint(array, pltpu.VMEM)
 
 
 def line_tables(count):
@@ -98,47 +109,145 @@
     return high, low
 
 
-def operator_kernel(k, nx, vec_ref, react_ref, low_ref, high_ref, inside_ref, table_ref, w_ref, gram_ref, field, react, both):
+def border_kernel(odd_ref, vec_ref, react_ref, inner_ref, outer_ref):
+    k, nx, plane = vec_ref.shape
+    odd = odd_ref[0]
+
+    def fill(ref, start):
+        for j in range(POWERS):
+            ref[j, :k, :] = vec_ref[:, start + j, :]
+            ref[j, k:, :] = jnp.broadcast_to(react_ref[start + j : start + j + 1, :], (8, plane))
+
+    @pl.when(odd == 0)
+    def _():
+        fill(inner_ref, nx - POWERS)
+        fill(outer_ref, 0)
+
+    @pl.when(odd != 0)
+    def _():
+        fill(inner_ref, 0)
+        fill(outer_ref, nx - POWERS)
+
+
+def borders(odd, vectors, reaction):
+    k, nx, plane = vectors.shape
+    shape = in_vmem(POWERS, k + 8, plane)
+    return pl.pallas_call(
+        border_kernel,
+        out_shape=(shape, shape),
+        in_specs=[pl.BlockSpec(memory_space=pltpu.SMEM), VMEM_SPEC, VMEM_SPEC],
+        out_specs=(VMEM_SPEC, VMEM_SPEC),
+        compiler_params=SMALL,
+        name="borders",
+    )(odd, vectors, reaction)
+
+
+def products(field, both, table, start, count):
+    k = field.shape[1]
+    n = count * k
+    one, two, three = split3(field[pl.ds(start, count)].reshape(n, PLANE))
+    parts = dot(jnp.concatenate([one, two, three], axis=0), table)
+    both[pl.ds(start, count)] = (parts[:n] + parts[n : 2 * n] + parts[2 * n :]).reshape(count, k, 2 * PLANE)
+
+
+def begin_kernel(vec_ref, table_ref, field, both):
+    k, nx, plane = vec_ref.shape
+    for x in range(nx):
+        field[x] = vec_ref[:, x, :]
+    table = table_ref[...]
+
+    def one_part(i, _):
+        products(field, both, table, 0, nx)
+        return 0
+
+    lax.fori_loop(0, 1, one_part, 0)
+
+
+def begin(vectors, table):
+    k, nx, plane = vectors.shape
+    return pl.pallas_call(
+        begin_kernel,
+        out_shape=(in_vmem(nx, k, plane), in_vmem(nx, k, 2 * plane)),
+        in_specs=[VMEM_SPEC, VMEM_SPEC],
+        out_specs=(VMEM_SPEC, VMEM_SPEC),
+        cost_estimate=pl.CostEstimate(flops=2 * 3 * nx * k * plane * 2 * plane, bytes_accessed=0, transcendentals=0),
+        compiler_params=SMALL,
+        name="begin",
+    )(vectors, table)
+
+
+def operator_kernel(k, nx, flags_ref, react_ref, inner_ref, outer_ref, table_ref, own_ref, own_both_ref, w_ref, gram_ref, field, both, react):
     halo = POWERS
     total = nx + 2 * halo
-    chunk = 2
-    for x in range(nx):
-        field[halo + x] = vec_ref[:, x, :]
-    for x in range(halo):
-        field[x] = low_ref[x, :k, :]
-        field[halo + nx + x] = high_ref[x, :k, :]
+    odd = flags_ref[0]
+    low_inside = flags_ref[1].astype(F32)
+    high_inside = flags_ref[2].astype(F32)
+    react[halo : halo + nx] = react_ref[...]
+
+    def fill(low_ref, high_ref):
+        field[0:halo] = low_ref[:, :k, :]
+        field[halo + nx : total] = high_ref[:, :k, :]
+        react[0:halo] = low_ref[:, k, :]
+        react[halo + nx : total] = high_ref[:, k, :]
+
+    @pl.when(odd == 0)
+    def _():
+        fill(outer_ref, inner_ref)
+
+    @pl.when(odd != 0)
+    def _():
+        fill(inner_ref, outer_ref)
+
     table = table_ref[...]
-    react[0:halo] = low_ref[:, k, :]
-    react[halo : halo + nx] = react_ref[...]
-    react[halo + nx : total] = high_ref[:, k, :]
-    low_inside = inside_ref[0]
-    high_inside = inside_ref[1]
-    for step in range(POWERS):
+
+    def combine(step, x, values, parts, offset):
+        value = (
+            parts[x - 1 - offset, :, :PLANE] + parts[x + 1 - offset, :, :PLANE] + parts[x - offset, :, PLANE:]
+        ) * (1.0 / 216.0) + react[pl.ds(x, 1), :] * values[x - offset]
+        if step < POWERS - 1:
+            keep = jnp.where(x < halo, low_inside, jnp.where(x >= halo + nx, high_inside, 1.0))
+            field[x] = value * keep
+        else:
+            w_ref[x - halo] = value
+        return 0
+
+    def edge(i, _):
+        products(field, both, table, i * (halo + nx), halo)
+        return 0
+
+    lax.fori_loop(0, 2, edge, 0)
+
+    def own_edge(i, _):
+        x = jnp.where(i < 2, i, nx - 4 + i)
+        field[halo + x] = own_ref[x]
+        both[halo + x] = own_both_ref[x]
+        return 0
+
+    lax.fori_loop(0, 4, own_edge, 0)
+
+    def outside(i, _):
+        x = jnp.where(i < halo, 1 + i, nx - 1 + i)
+        return combine(0, x, field, both, 0)
+
+    lax.fori_loop(0, 2 * halo, outside, 0)
+
+    def inside(x, _):
+        return combine(0, x, own_ref, own_both_ref, halo)
+
+    lax.fori_loop(halo + 1, halo + nx - 1, inside, 0, unroll=7)
+    for step in range(1, POWERS):
         first, last = step, total - step
-        chunk = (22,20,18)[step]
 
         def product(i, _):
-            x = first + chunk * i
-            one, two, three = split3(field[pl.ds(x, chunk)].reshape(chunk * k, PLANE))
-            parts = dot(jnp.concatenate([one, two, three], axis=0), table)
-            n = chunk * k
-            both[pl.ds(x, chunk)] = (parts[:n] + parts[n : 2 * n] + parts[2 * n :]).reshape(chunk, k, 2 * PLANE)
+            products(field, both, table, first, last - first)
             return 0
 
-        lax.fori_loop(0, (last - first) // chunk, product, 0)
-
-        def combine(x, _):
-            value = (
-                both[x - 1, :, :PLANE] + both[x + 1, :, :PLANE] + both[x, :, PLANE:]
-            ) * (1.0 / 216.0) + react[pl.ds(x, 1), :] * field[x]
-            if step < POWERS - 1:
-                keep = jnp.where(x < halo, low_inside, jnp.where(x >= halo + nx, high_inside, 1.0))
-                field[x] = value * keep
-            else:
-                w_ref[x - halo] = value
-            return 0
-
-        lax.fori_loop(first + 1, last - 1, combine, 0, unroll=4)
+        lax.fori_loop(0, 1, product, 0)
+
+        def later(x, _):
+            return combine(step, x, field, both, 0)
+
+        lax.fori_loop(first + 1, last - 1, later, 0, unroll=(last - first - 2) // 2)
     peak = jnp.abs(w_ref[0])
     for x in range(1, nx):
         peak = jnp.maximum(peak, jnp.abs(w_ref[x]))
@@ -184,26 +293,24 @@
     gram_ref[:, 0, :] = jnp.concatenate([high * row * column, err * row * column], axis=1)
 
 
-def operator_and_gram(vectors, reaction, low, high, inside):
-    k, nx, plane = vectors.shape
+def operator_and_gram(flags, reaction, inner, outer, table, own, own_both):
+    nx, k, plane = own.shape
     total = nx + 2 * POWERS
-    vmem = pl.BlockSpec(memory_space=pltpu.VMEM)
     smem = pl.BlockSpec(memory_space=pltpu.SMEM)
     return pl.pallas_call(
         lambda *refs: operator_kernel(k, nx, *refs),
-        out_shape=(
-            jax.ShapeDtypeStruct((nx, k, plane), F32),
-            jax.ShapeDtypeStruct((k, 1, 2 * k), F32),
-        ),
-        in_specs=[vmem, vmem, vmem, vmem, smem, vmem],
-        out_specs=(vmem, vmem),
+        out_shape=(in_vmem(nx, k, plane), in_vmem(k, 1, 2 * k)),
+        in_specs=[smem] + [VMEM_SPEC] * 6,
+        out_specs=(VMEM_SPEC, VMEM_SPEC),
         scratch_shapes=[
             pltpu.VMEM((total, k, plane), F32),
+            pltpu.VMEM((total, k, 2 * plane), F32),
             pltpu.VMEM((total, plane), F32),
-            pltpu.VMEM((total, k, 2 * plane), F32),
         ],
+        cost_estimate=pl.CostEstimate(flops=2 * 3 * 44 * k * plane * 2 * plane, bytes_accessed=0, transcendentals=0),
+        compiler_params=SMALL,
         name="operator_gram",
-    )(vectors, reaction, low, high, inside, jnp.asarray(tables()))
+    )(flags, reaction, vmem(inner), vmem(outer), table, vmem(own), vmem(own_both))
 
 
 def pair_sum_kernel(parts_ref, out_ref):
@@ -225,11 +332,12 @@
 def pair_sum(parts, copies):
     return pl.pallas_call(
         pair_sum_kernel,
-        out_shape=jax.ShapeDtypeStruct((copies, 1, parts.shape[2]), F32),
-        in_specs=[pl.BlockSpec(memory_space=pltpu.VMEM)],
-        out_specs=pl.BlockSpec(memory_space=pltpu.VMEM),
+        out_shape=in_vmem(copies, 1, parts.shape[2]),
+        in_specs=[VMEM_SPEC],
+        out_specs=VMEM_SPEC,
+        compiler_params=SMALL,
         name="pair_sum",
-    )(parts)
+    )(vmem(parts))
 
 
 def sum_over_devices(gram):
@@ -364,16 +472,15 @@
 
 def factor(gram, scale):
     k = gram.shape[0]
-    vmem = pl.BlockSpec(memory_space=pltpu.VMEM)
-    square = jax.ShapeDtypeStruct((k, k), F32)
     return pl.pallas_call(
         lambda *refs: factor_kernel(scale, *refs),
-        out_shape=(square, square, square),
-        in_specs=[vmem],
-        out_specs=(vmem, vmem, vmem),
+        out_shape=(in_vmem(k, k), in_vmem(k, k), jax.ShapeDtypeStruct((k, k), F32)),
+        in_specs=[VMEM_SPEC],
+        out_specs=(VMEM_SPEC, VMEM_SPEC, VMEM_SPEC),
         scratch_shapes=[pltpu.VMEM((k, k), F32)],
+        compiler_params=SMALL,
         name="factor",
-    )(gram)
+    )(vmem(gram))
 
 
 def basis_kernel(w_ref, high_ref, low_ref, out_ref):
@@ -388,34 +495,29 @@
 
 def basis_of(w, high, low):
     nx, k, plane = w.shape
-    vmem = pl.BlockSpec(memory_space=pltpu.VMEM)
     return pl.pallas_call(
         basis_kernel,
         out_shape=jax.ShapeDtypeStruct((k, nx, plane), F32),
-        in_specs=[vmem, vmem, vmem],
-        out_specs=vmem,
+        in_specs=[VMEM_SPEC] * 3,
+        out_specs=VMEM_SPEC,
+        compiler_params=SMALL,
         name="basis",
-    )(w, high, low)
-
-
-def border(vectors, reaction):
-    rows = jnp.swapaxes(vectors, 0, 1)
-    react = jnp.broadcast_to(reaction[:, None], (reaction.shape[0], 8, reaction.shape[1]))
-    return jnp.concatenate([rows, react], axis=1)
+    )(vmem(w), vmem(high), vmem(low))
 
 
 def per_device(vectors, reaction):
     k, nx, plane = vectors.shape
     peers = lax.axis_size(SFC_SUB)
     me = lax.axis_index(SFC_SUB)
-    up = [(i, i + 1) for i in range(peers - 1)]
-    down = [(i + 1, i) for i in range(peers - 1)]
-    last = border(vectors[:, nx - POWERS :], reaction[nx - POWERS :])
-    leading = border(vectors[:, :POWERS], reaction[:POWERS])
-    low = lax.ppermute(last, SFC_SUB, up)
-    high = lax.ppermute(leading, SFC_SUB, down)
-    inside = jnp.stack([me > 0, me < peers - 1]).astype(F32)
-    w, gram = operator_and_gram(vectors, reaction, low, high, inside)
+    flags = jnp.stack([me % 2, (me > 0).astype(me.dtype), (me < peers - 1).astype(me.dtype)])
+    inner, outer = borders(flags, vectors, reaction)
+    across = [(i, i + 1) for i in range(1, peers - 1, 2)]
+    within = [(i, i + 1) for i in range(0, peers, 2)]
+    outer = lax.ppermute(outer, SFC_SUB, across + [(b, a) for a, b in across])
+    inner = lax.ppermute(inner, SFC_SUB, within + [(b, a) for a, b in within])
+    table = jnp.asarray(tables())
+    field, both = begin(vectors, table)
+    w, gram = operator_and_gram(flags, reaction, inner, outer, table, field, both)
     gram = sum_over_devices(gram)
     high, low, upper = factor(gram, math.sqrt(peers * nx * plane))
     return basis_of(w, high, low), upper

time: 106 us -> 96 us (0.906)
  blocking collectives: 60.9 us -> 54.2 us
  Pallas kernels: 22 us -> 16.6 us
  waiting for transfers between devices: 0.51 us -> 1.93 us
  local copies, waits for them, and re-layouts: 2.96 us -> 4.12 us
    pallas_call x4 -> x6, Pallas kernels: 18.8 us -> 14.7 us  [the longest x1 6.47 us: factor(): pl.pallas_call(lambda *refs: factor_kernel(scale, *refs), out_shape=(in_v...]
    all_to_all x1, blocking collectives: 15 us -> 11.5 us  [sum_over_devices(): rows = lax.all_to_all(gram, NEAR, 0, 0)]
    unnamed x6 -> x12, local copies, waits for them, and re-layouts: 0.94 us -> 4.12 us
    all_to_all x1, blocking collectives: 29.8 us -> 27.8 us  [sum_over_devices(): mine = pair_sum(lax.all_to_all(mine, FAR, 0, 0), near)]
    slice x2 -> x0, local copies, waits for them, and re-layouts: 2.01 us -> none  [per_device(): leading = border(vectors[:, :POWERS], reaction[:POWERS])]
    ppermute x2, waiting for transfers between devices: 0.51 us -> 1.93 us  [the longest x1 1.92 us: per_device(): outer = lax.ppermute(outer, SFC_SUB, across + [(b, a) for a, b in across])]
    all_to_all x1, blocking collectives: 16.1 us -> 14.8 us  [sum_over_devices(): return lax.all_to_all(mine, NEAR, 0, 0)]
    pallas_call x1, Pallas kernels: 3.13 us -> 1.88 us  [basis_of(): pl.pallas_call(basis_kernel, out_shape=jax.ShapeDtypeStruct((k, nx, plane...]
  transfers between devices with their start and end apart: 2 -> 2, of which waited for: 1 -> 1; matrix products, arithmetic and copies ran while one was open for 1% -> 0% of each run, Pallas kernels for 0% -> 1%
where the time goes in v3:
time: 96 us; the launch traced here: 95.6 us
  blocking collectives  54.2 us (56%)
  starting transfers between devices  17.9 us (19%)
  Pallas kernels  16.6 us (17%)
  local copies, waits for them, and re-layouts  4.12 us (4%)
  waiting for transfers between devices  1.93 us (2%)
    all_to_all x1, blocking collectives, sum_over_devices(): mine = pair_sum(lax.all_to_all(mine, FAR, 0, 0), near)  27.8 us
    ppermute x1, starting transfers between devices, per_device(): inner = lax.ppermute(inner, SFC_SUB, within + [(b, a) for a, b in within])  16 us
    all_to_all x1, blocking collectives, sum_over_devices(): return lax.all_to_all(mine, NEAR, 0, 0)  14.8 us
    all_to_all x1, blocking collectives, sum_over_devices(): rows = lax.all_to_all(gram, NEAR, 0, 0)  11.5 us
    pallas_call x1, Pallas kernels, factor(): pl.pallas_call(lambda *refs: factor_kernel(scale, *refs), out_shape=(in_v...  6.47 us
    pallas_call x1, Pallas kernels, operator_and_gram(): pl.pallas_call(lambda *refs: operator_kernel(k, nx, *refs), out_shape=(in...  6 us
    unnamed x12, local copies, waits for them, and re-layouts  4.12 us
    ppermute x1, waiting for transfers between devices, per_device(): outer = lax.ppermute(outer, SFC_SUB, across + [(b, a) for a, b in across])  1.92 us
  transfers between devices with their start and end apart: 2, of which 1 were waited for; matrix products, arithmetic and copies ran while one was open for 0% of the time, Pallas kernels for 1%

profile of v3, /device:TPU:1, one launch (start us, length us, event | category | flops | bytes accessed | tf_op | source)
XLA Modules:
  0.0 95.6 jit_solution(18424078440770420206)
XLA Ops:
  0.6 0.0 copy-start.3
  0.7 0.1 pad_add_fusion.odd_ref.refs_0_
  0.7 0.0 copy-start
  0.7 1.2 %copy-done = f32[64,16,256]{2,1,0:T(8,128)S(1)} copy-done((f32[64,16,256]{2,1,0:T(8,128)S(1)}, f32[64,16,256]{2,1,0:T(8,128)}, u32[]{:S(2)}) %copy-start) | copy-done | bytes 1048600
  2.0 0.7 copy-done.2
  2.7 0.7 borders.1
  3.4 16.0 %collective-permute-start = (f32[3,72,256]{2,1,0:T(8,128)S(1)}, f32[3,72,256]{2,1,0:T(8,128)S(1)}, u32[]{:S(2)}, u32[]{:S(2)}) collective-permute-start(f32[3,72,256]{2,1,0:T(8,128)S(1)} %get-tuple-element.11), channel_id=1, source_target_pairs={{0,1},{2,3},{4,5},{6,7},{8,9},{10,11},{12,13},{14,15},{16,17},{18,... | collective-permute-start | bytes 663560 | tf_op jit(solution)/shard_map/ppermute | solution.py:517
  19.4 1.9 %collective-permute-start.1 = (f32[3,72,256]{2,1,0:T(8,128)S(1)}, f32[3,72,256]{2,1,0:T(8,128)S(1)}, u32[]{:S(2)}, u32[]{:S(2)}) collective-permute-start(f32[3,72,256]{2,1,0:T(8,128)S(1)} %get-tuple-element.12), channel_id=1, source_target_pairs={{1,2},{3,4},{5,6},{7,8},{9,10},{11,12},{13,14},{15,16},{17,18},{19... | collective-permute-start | bytes 663560 | tf_op jit(solution)/shard_map/ppermute | solution.py:516
  21.4 0.0 copy-start.1
  21.4 1.2 %copy-done.1 = f32[64,16,256]{2,1,0:T(8,128)S(1)} copy-done((f32[64,16,256]{2,1,0:T(8,128)S(1)}, f32[64,16,256]{2,1,0:T(8,128)}, u32[]{:S(2)}) %copy-start.1) | copy-done | bytes 1048600
  22.6 0.9 copy-done.4
  23.5 1.2 %begin.1 = (f32[16,64,256]{2,1,0:T(8,128)S(1)}, f32[16,64,512]{2,1,0:T(8,128)S(1)}) custom-call(f32[64,16,256]{2,1,0:T(8,128)S(1)} %copy-done.1, bf16[256,512]{1,0:T(8,128)(2,1)S(1)} %copy-done.4), custom_call_target="tpu_custom_call" | custom-call | flops 805306368 | tf_op jit(solution)/shard_map/begin/pallas_call | solution.py:168
  24.8 0.0 collective-permute-done.refs_2_
  24.8 1.9 %collective-permute-done.1.refs_3_ = f32[3,72,256]{2,1,0:T(8,128)S(1)} collective-permute-done((f32[3,72,256]{2,1,0:T(8,128)S(1)}, f32[3,72,256]{2,1,0:T(8,128)S(1)}, u32[]{:S(2)}, u32[]{:S(2)}) %collective-permute-start.1) | collective-permute-done | bytes 221216 | tf_op jit(solution)/shard_map/ppermute | solution.py:516
  26.7 0.0 copy-done.3
  26.7 0.0 copy-done.5
  26.7 6.0 %operator_gram.1 = (f32[16,64,256]{2,1,0:T(8,128)S(1)}, f32[64,1,128]{2,1,0:T(1,128)S(1)}) custom-call(s32[3]{0:T(128)S(1)} %pad_add_fusion.odd_ref.refs_0_, f32[16,256]{1,0:T(8,128)S(1)} %copy-done.3, f32[3,72,256]{2,1,0:T(8,128)S(1)} %collective-permute-done.refs_2_, f32[3,72,256]{2,1,0:T(8,128)S(1)} %collective-permute-done.1.refs_3_, ...), custom_call_target="tpu_custom_call" | custom-call | flops 2214592512 | tf_op jit(solution)/shard_map/operator_gram/pallas_call | solution.py:300
  32.7 11.5 %all_to_all.15.parts_ref = f32[64,1,128]{2,1,0:T(1,128)S(1)} all-to-all(f32[64,1,128]{2,1,0:T(1,128)S(1)} %get-tuple-element.16), channel_id=1, replica_groups=mesh['sfc_0'=16,'sfc_1'=8,'sub_0'=4,'sub_1'=2] {'sfc_1','sub_0','sub_1'}, dimensions={0} | all-to-all | bytes 65536 | tf_op jit(solution)/shard_map/all_to_all | solution.py:346
  44.2 0.2 pair_sum.2
  44.4 27.8 %all_to_all.16.parts_ref = f32[16,1,128]{2,1,0:T(1,128)S(1)} all-to-all(f32[16,1,128]{2,1,0:T(1,128)S(1)} %pair_sum.2), channel_id=1, replica_groups=mesh['sfc_0'=16,'sfc_1'=8,'sub_0'=4,'sub_1'=2] {'sfc_0'}, dimensions={0} | all-to-all | bytes 16384 | tf_op jit(solution)/shard_map/all_to_all | solution.py:348
  72.2 0.2 pair_sum.3
  72.4 14.8 %all_to_all.17.refs_0_ = f32[64,1,128]{2,1,0:T(1,128)S(1)} all-to-all(f32[64,1,128]{2,1,0:T(1,128)S(1)} %pair_sum.3), channel_id=1, replica_groups=mesh['sfc_0'=16,'sfc_1'=8,'sub_0'=4,'sub_1'=2] {'sfc_1','sub_0','sub_1'}, dimensions={0} | all-to-all | bytes 65536 | tf_op jit(solution)/shard_map/all_to_all | solution.py:349
  87.2 6.5 %factor.1 = (f32[64,64]{1,0:T(8,128)S(1)}, f32[64,64]{1,0:T(8,128)S(1)}, f32[64,64]{1,0:T(8,128)}) custom-call(f32[64,1,128]{2,1,0:T(1,128)S(1)} %all_to_all.17.refs_0_), custom_call_target="tpu_custom_call" | custom-call | tf_op jit(solution)/shard_map/factor/pallas_call | solution.py:475
  93.7 1.9 %basis.1 = f32[64,16,256]{2,1,0:T(8,128)} custom-call(f32[16,64,256]{2,1,0:T(8,128)S(1)} %get-tuple-element.15.w_ref, f32[64,64]{1,0:T(8,128)S(1)} %get-tuple-element.17.high_ref, f32[64,64]{1,0:T(8,128)S(1)} %get-tuple-element.18.low_ref), custom_call_target="tpu_custom_call" | custom-call | tf_op jit(solution)/shard_map/basis/pallas_call | solution.py:498
  (3 shorter events, 0.0 us)
Async XLA Ops:
  0.6 26.1 %copy-start.3 = (f32[16,256]{1,0:T(8,128)S(1)}, f32[16,256]{1,0:T(8,128)}, u32[]{:S(2)}) copy-start(f32[16,256]{1,0:T(8,128)} %refs_1_.1) | copy-start | bytes 49156
  0.7 1.2 %copy-start = (f32[64,16,256]{2,1,0:T(8,128)S(1)}, f32[64,16,256]{2,1,0:T(8,128)}, u32[]{:S(2)}) copy-start(f32[64,16,256]{2,1,0:T(8,128)} %vec_ref.3) | copy-start | bytes 3145732
  2.0 0.7 copy-start.2
  2.7 24.0 %copy-start.5 = (bf16[256,512]{1,0:T(8,128)(2,1)S(1)}, bf16[256,512]{1,0:T(8,128)(2,1)}, u32[]{:S(2)}) copy-start(bf16[256,512]{1,0:T(8,128)(2,1)} %constant.40.clone.table_ref.refs_4_) | copy-start | bytes 786436
  3.4 21.4 %collective-permute-start = (f32[3,72,256]{2,1,0:T(8,128)S(1)}, f32[3,72,256]{2,1,0:T(8,128)S(1)}, u32[]{:S(2)}, u32[]{:S(2)}) collective-permute-start(f32[3,72,256]{2,1,0:T(8,128)S(1)} %get-tuple-element.11), channel_id=1, source_target_pairs={{0,1},{2,3},{4,5},{6,7},{8,9},{10,11},{12,13},{14,15},{16,17},{18,... | collective-permute-start | bytes 663560 | tf_op jit(solution)/shard_map/ppermute | solution.py:517
  19.4 7.3 %collective-permute-start.1 = (f32[3,72,256]{2,1,0:T(8,128)S(1)}, f32[3,72,256]{2,1,0:T(8,128)S(1)}, u32[]{:S(2)}, u32[]{:S(2)}) collective-permute-start(f32[3,72,256]{2,1,0:T(8,128)S(1)} %get-tuple-element.12), channel_id=1, source_target_pairs={{1,2},{3,4},{5,6},{7,8},{9,10},{11,12},{13,14},{15,16},{17,18},{19... | collective-permute-start | bytes 663560 | tf_op jit(solution)/shard_map/ppermute | solution.py:516
  21.4 1.2 %copy-start.1 = (f32[64,16,256]{2,1,0:T(8,128)S(1)}, f32[64,16,256]{2,1,0:T(8,128)}, u32[]{:S(2)}) copy-start(f32[64,16,256]{2,1,0:T(8,128)} %vec_ref.3) | copy-start | bytes 3145732
  22.6 0.9 copy-start.4

commit v4 on v3

--- a/solution.py
+++ b/solution.py
@@ -31,6 +31,10 @@
 
 def vmem(array):
     return pltpu.with_memory_space_constraint(array, pltpu.VMEM)
+
+
+def hbm(array):
+    return pltpu.with_memory_space_constraint(array, pltpu.HBM)
 
 
 def line_tables(count):
@@ -109,37 +113,56 @@
     return high, low
 
 
-def border_kernel(odd_ref, vec_ref, react_ref, inner_ref, outer_ref):
+def border_kernel(odd_ref, vec_ref, react_ref, table_ref, inner_ref, outer_ref, own_ref, own_react_ref, own_table_ref, sems):
     k, nx, plane = vec_ref.shape
+    parts = 4
+    copies = []
+    for part in range(parts):
+        rows = pl.ds(part * (k // parts), k // parts)
+        copies.append(pltpu.make_async_copy(vec_ref.at[rows], own_ref.at[rows], sems.at[part]))
+    copies.append(pltpu.make_async_copy(react_ref, own_react_ref, sems.at[parts]))
+    copies.append(pltpu.make_async_copy(table_ref, own_table_ref, sems.at[parts + 1]))
+    for copy in copies:
+        copy.start()
+    copies[-2].wait()
     odd = odd_ref[0]
 
-    def fill(ref, start):
+    def fill(ref, start, rows):
         for j in range(POWERS):
-            ref[j, :k, :] = vec_ref[:, start + j, :]
-            ref[j, k:, :] = jnp.broadcast_to(react_ref[start + j : start + j + 1, :], (8, plane))
-
-    @pl.when(odd == 0)
-    def _():
-        fill(inner_ref, nx - POWERS)
-        fill(outer_ref, 0)
-
-    @pl.when(odd != 0)
-    def _():
-        fill(inner_ref, 0)
-        fill(outer_ref, nx - POWERS)
-
-
-def borders(odd, vectors, reaction):
-    k, nx, plane = vectors.shape
+            ref[j, rows, :] = own_ref[rows, start + j, :]
+            if rows.start == 0:
+                ref[j, k:, :] = jnp.broadcast_to(own_react_ref[start + j : start + j + 1, :], (8, plane))
+
+    for part in range(parts):
+        rows = pl.ds(part * (k // parts), k // parts)
+        copies[part].wait()
+
+        @pl.when(odd == 0)
+        def _():
+            fill(inner_ref, nx - POWERS, rows)
+            fill(outer_ref, 0, rows)
+
+        @pl.when(odd != 0)
+        def _():
+            fill(inner_ref, 0, rows)
+            fill(outer_ref, nx - POWERS, rows)
+
+    copies[-1].wait()
+
+
+def borders(odd, vectors, reaction, table):
+    k, _, plane = vectors.shape
     shape = in_vmem(POWERS, k + 8, plane)
+    anywhere = pl.BlockSpec(memory_space=pltpu.HBM)
     return pl.pallas_call(
         border_kernel,
-        out_shape=(shape, shape),
-        in_specs=[pl.BlockSpec(memory_space=pltpu.SMEM), VMEM_SPEC, VMEM_SPEC],
-        out_specs=(VMEM_SPEC, VMEM_SPEC),
+        out_shape=(shape, shape, in_vmem(*vectors.shape), in_vmem(*reaction.shape), pltpu.VMEM(table.shape, table.dtype)),
+        in_specs=[pl.BlockSpec(memory_space=pltpu.SMEM), anywhere, anywhere, anywhere],
+        out_specs=(VMEM_SPEC,) * 5,
+        scratch_shapes=[pltpu.SemaphoreType.DMA((6,))],
         compiler_params=SMALL,
         name="borders",
-    )(odd, vectors, reaction)
+    )(odd, hbm(vectors), hbm(reaction), hbm(table))
 
 
 def products(field, both, table, start, count):
@@ -151,7 +174,7 @@
 
 
 def begin_kernel(vec_ref, table_ref, field, both):
-    k, nx, plane = vec_ref.shape
+    _, nx, _ = vec_ref.shape
     for x in range(nx):
         field[x] = vec_ref[:, x, :]
     table = table_ref[...]
@@ -173,7 +196,7 @@
         cost_estimate=pl.CostEstimate(flops=2 * 3 * nx * k * plane * 2 * plane, bytes_accessed=0, transcendentals=0),
         compiler_params=SMALL,
         name="begin",
-    )(vectors, table)
+    )(vmem(vectors), vmem(table))
 
 
 def operator_kernel(k, nx, flags_ref, react_ref, inner_ref, outer_ref, table_ref, own_ref, own_both_ref, w_ref, gram_ref, field, both, react):
@@ -310,7 +333,7 @@
         cost_estimate=pl.CostEstimate(flops=2 * 3 * 44 * k * plane * 2 * plane, bytes_accessed=0, transcendentals=0),
         compiler_params=SMALL,
         name="operator_gram",
-    )(flags, reaction, vmem(inner), vmem(outer), table, vmem(own), vmem(own_both))
+    )(flags, vmem(reaction), vmem(inner), vmem(outer), vmem(table), vmem(own), vmem(own_both))
 
 
 def pair_sum_kernel(parts_ref, out_ref):
@@ -376,9 +399,9 @@
 
 def eliminate(square):
     k = square.shape[0]
-    row = lax.broadcasted_iota(jnp.int32, (k, 2 * k), 0)
-    lane = lax.broadcasted_iota(jnp.int32, (k, 2 * k), 1)
-    eye = (row[:, :k] == lane[:, :k]).astype(F32)
+    row = lax.broadcasted_iota(jnp.int32, (k, k), 0)
+    lane = lax.broadcasted_iota(jnp.int32, (k, k), 1)
+    eye = (row == lane).astype(F32)
     block = 8
     work = jnp.concatenate([square, eye], axis=1)
     done = []
@@ -386,16 +409,23 @@
         rows = work.shape[0]
         columns = [jnp.broadcast_to(work[:, start + a : start + a + 1], (rows, 2 * k)) for a in range(block)]
         below = lax.broadcasted_iota(jnp.int32, (rows, 2 * k), 0)
-        for a in range(block):
-            inverse = 1.0 / columns[a][a : a + 1, :]
-            many = jnp.where(below > a, columns[a] * inverse, 0.0)
-            for b in range(a + 1, block):
-                columns[b] = columns[b] - many * columns[b][a : a + 1, :]
-            work = work - many * work[a : a + 1, :]
+        for a in range(0, block, 2):
+            one, two = columns[a], columns[a + 1]
+            p, q, r = one[a : a + 1, :], two[a : a + 1, :], two[a + 1 : a + 2, :]
+            inverse = 1.0 / (p * r - q * q)
+            first = jnp.where(below > a + 1, (one * r - two * q) * inverse, 0.0)
+            second = jnp.where(below > a + 1, (two * p - one * q) * inverse, 0.0)
+            for b in range(a + 2, block):
+                columns[b] = columns[b] - (first * columns[b][a : a + 1, :] + second * columns[b][a + 1 : a + 2, :])
+            work = work - (first * work[a : a + 1, :] + second * work[a + 1 : a + 2, :])
         done.append(work[:block])
         work = work[block:]
     work = jnp.concatenate(done, axis=0)
     pivot = jnp.sum(work[:, :k] * eye, axis=1, keepdims=True)
+    beside = jnp.sum(jnp.where((row == lane + 1) & (row % 2 == 1), work[:, :k], 0.0), axis=1, keepdims=True)
+    ratio = beside / pltpu.roll(jnp.broadcast_to(pivot, (k, 2 * k)), 1, 0)
+    work = work - ratio * pltpu.roll(work, 1, 0)
+    pivot = pivot - ratio[:, :k] * beside
     return work[:, k:] * lax.rsqrt(pivot)
 
 
@@ -403,17 +433,21 @@
     def lower(value):
         return jnp.where(strict, value, jnp.where(half, 0.5 * value, 0.0))
 
+    def pair(value):
+        one = value.astype(BF16)
+        return one, (value - one.astype(F32)).astype(BF16)
+
+    d1, d2 = pair(delta)
+    right = jnp.concatenate([d1, d2, d1], axis=0)
     y = -lower(delta)
-    for _ in range(3):
-        a = dot_full(y, delta)
-        outer = y + a
-        y1, y2, y3 = split3(y)
-        o1, o2, o3 = split3(outer)
-        square = dot_t(
-            jnp.concatenate([o1, o1, o2, o1, o2, o3], axis=1), jnp.concatenate([y1, y2, y1, y3, y2, y1], axis=1)
-        )
-        error = lower(delta + (y + y.T) + (a + a.T) + square)
-        y = y - error - dot_full(error, y)
+    for _ in range(2):
+        y1, y2 = pair(y)
+        outer = y + dot(jnp.concatenate([y1, y1, y2], axis=1), right)
+        o1, o2 = pair(outer)
+        square = dot_t(jnp.concatenate([o1, o1, o2], axis=1), jnp.concatenate([y1, y2, y1], axis=1))
+        error = lower(delta + outer + outer.T + square)
+        e1, e2 = pair(error)
+        y = y - error - dot_of_stack([e1, e1, e2], [y1, y2, y1])
     return y
 
 
@@ -450,7 +484,7 @@
     low = low * unit
     delta = jnp.where(eye, high - 1.0, high) + low
     worst = jnp.max(jnp.abs(delta))
-    small = worst < 2.0**-8
+    small = worst < 2.0**-9
 
     @pl.when(small)
     def _():
@@ -483,14 +517,22 @@
     )(vmem(gram))
 
 
-def basis_kernel(w_ref, high_ref, low_ref, out_ref):
+def basis_kernel(w_ref, high_ref, low_ref, out_ref, result, sems):
+    _, nx, _ = result.shape
     p1, p2, p3 = split3(high_ref[...])
     p4 = low_ref[...].astype(BF16)
     left = jnp.concatenate([p1, p1, p1, p2, p2, p3, p4], axis=1)
-    for x in range(w_ref.shape[0]):
+    copies = []
+    for x in range(nx):
         w1, w2, w3 = split3(w_ref[x])
         right = jnp.concatenate([w3, w2, w1, w2, w1, w1, w1], axis=0)
-        out_ref[:, x, :] = dot(left, right)
+        result[:, x, :] = dot(left, right)
+        if (x + 1) % 8 == 0:
+            rows = pl.ds(x - 7, 8)
+            copies.append(pltpu.make_async_copy(result.at[:, rows, :], out_ref.at[:, rows, :], sems.at[x // 8]))
+            copies[-1].start()
+    for copy in copies:
+        copy.wait()
 
 
 def basis_of(w, high, low):
@@ -499,23 +541,23 @@
         basis_kernel,
         out_shape=jax.ShapeDtypeStruct((k, nx, plane), F32),
         in_specs=[VMEM_SPEC] * 3,
-        out_specs=VMEM_SPEC,
+        out_specs=pl.BlockSpec(memory_space=pltpu.HBM),
+        scratch_shapes=[pltpu.VMEM((k, nx, plane), F32), pltpu.SemaphoreType.DMA((nx // 8,))],
         compiler_params=SMALL,
         name="basis",
     )(vmem(w), vmem(high), vmem(low))
 
 
-def per_device(vectors, reaction):
-    k, nx, plane = vectors.shape
+def device_program(vectors, reaction):
+    _, nx, plane = vectors.shape
     peers = lax.axis_size(SFC_SUB)
     me = lax.axis_index(SFC_SUB)
     flags = jnp.stack([me % 2, (me > 0).astype(me.dtype), (me < peers - 1).astype(me.dtype)])
-    inner, outer = borders(flags, vectors, reaction)
+    inner, outer, vectors, reaction, table = borders(flags, vectors, reaction, jnp.asarray(tables()))
     across = [(i, i + 1) for i in range(1, peers - 1, 2)]
     within = [(i, i + 1) for i in range(0, peers, 2)]
     outer = lax.ppermute(outer, SFC_SUB, across + [(b, a) for a, b in across])
     inner = lax.ppermute(inner, SFC_SUB, within + [(b, a) for a, b in within])
-    table = jnp.asarray(tables())
     field, both = begin(vectors, table)
     w, gram = operator_and_gram(flags, reaction, inner, outer, table, field, both)
     gram = sum_over_devices(gram)
@@ -527,6 +569,4 @@
     torus = Mesh(mesh.devices.reshape(16, 8, 4, 2), ("sfc_0", "sfc_1", "sub_0", "sub_1"))
     in_specs = (P(None, SFC_SUB, None), P(SFC_SUB, None))
     out_specs = (P(None, SFC_SUB, None), P())
-    return jax.shard_map(
-        per_device, mesh=torus, in_specs=in_specs, out_specs=out_specs, check_vma=False
-    )
+    return jax.shard_map(device_program, mesh=torus, in_specs=in_specs, out_specs=out_specs, check_vma=False)

time: 96 us -> 94.1 us (0.980)
  local copies, waits for them, and re-layouts: 4.12 us -> 0 us
  waiting for transfers between devices: 1.93 us -> 4.1 us
    unnamed x12 -> x0, local copies, waits for them, and re-layouts: 4.12 us -> none
    ppermute x2, waiting for transfers between devices: 1.93 us -> 4.1 us  [the longest x1 4.1 us: device_program(): outer = lax.ppermute(outer, SFC_SUB, across + [(b, a) for a, b in across])]
    pallas_call x1, Pallas kernels: 0.71 us -> 1.88 us  [borders(): pl.pallas_call(border_kernel, out_shape=(shape, shape, in_vmem(*vectors.s...]
where the time goes in v4:
time: 94.1 us; the launch traced here: 93.9 us
  blocking collectives  54.2 us (58%)
  starting transfers between devices  17.9 us (19%)
  Pallas kernels  16.9 us (18%)
  waiting for transfers between devices  4.1 us (4%)
    all_to_all x1, blocking collectives, sum_over_devices(): mine = pair_sum(lax.all_to_all(mine, FAR, 0, 0), near)  27.8 us
    ppermute x1, starting transfers between devices, device_program(): inner = lax.ppermute(inner, SFC_SUB, within + [(b, a) for a, b in within])  16 us
    all_to_all x1, blocking collectives, sum_over_devices(): return lax.all_to_all(mine, NEAR, 0, 0)  14.8 us
    all_to_all x1, blocking collectives, sum_over_devices(): rows = lax.all_to_all(gram, NEAR, 0, 0)  11.5 us
    pallas_call x1, Pallas kernels, operator_and_gram(): pl.pallas_call(lambda *refs: operator_kernel(k, nx, *refs), out_shape=(in...  6 us
    pallas_call x1, Pallas kernels, factor(): pl.pallas_call(lambda *refs: factor_kernel(scale, *refs), out_shape=(in_v...  5.7 us
    ppermute x1, waiting for transfers between devices, device_program(): outer = lax.ppermute(outer, SFC_SUB, across + [(b, a) for a, b in across])  4.1 us
    ppermute x1, starting transfers between devices, device_program(): outer = lax.ppermute(outer, SFC_SUB, across + [(b, a) for a, b in across])  1.92 us
  transfers between devices with their start and end apart: 2, of which 1 were waited for; matrix products, arithmetic and copies ran while one was open for 0% of the time, Pallas kernels for 1%

profile of v4, /device:TPU:1, one launch (start us, length us, event | category | flops | bytes accessed | tf_op | source)
XLA Modules:
  0.0 93.9 jit_solution(16216740891527074059)
XLA Ops:
  0.6 0.1 pad_add_fusion.odd_ref.refs_0_
  0.7 1.9 %borders.1 = (f32[3,72,256]{2,1,0:T(8,128)S(1)}, f32[3,72,256]{2,1,0:T(8,128)S(1)}, f32[64,16,256]{2,1,0:T(8,128)S(1)}, f32[16,256]{1,0:T(8,128)S(1)}, bf16[256,512]{1,0:T(8,128)(2,1)S(1)}) custom-call(s32[3]{0:T(128)S(1)} %pad_add_fusion.odd_ref.refs_0_, f32[64,16,256]{2,1,0:T(8,128)} %vec_ref.1, f32[16,256]{1,0:T(8,128)} %react_ref.1, ...), custom_call_target="tpu_custom_call" | custom-call | tf_op jit(solution)/shard_map/borders/pallas_call | solution.py:157
  2.6 16.0 %collective-permute-start = (f32[3,72,256]{2,1,0:T(8,128)S(1)}, f32[3,72,256]{2,1,0:T(8,128)S(1)}, u32[]{:S(2)}, u32[]{:S(2)}) collective-permute-start(f32[3,72,256]{2,1,0:T(8,128)S(1)} %get-tuple-element.15), channel_id=1, source_target_pairs={{0,1},{2,3},{4,5},{6,7},{8,9},{10,11},{12,13},{14,15},{16,17},{18,... | collective-permute-start | bytes 663560 | tf_op jit(solution)/shard_map/ppermute | solution.py:560
  18.6 1.9 %collective-permute-start.1 = (f32[3,72,256]{2,1,0:T(8,128)S(1)}, f32[3,72,256]{2,1,0:T(8,128)S(1)}, u32[]{:S(2)}, u32[]{:S(2)}) collective-permute-start(f32[3,72,256]{2,1,0:T(8,128)S(1)} %get-tuple-element.16), channel_id=1, source_target_pairs={{1,2},{3,4},{5,6},{7,8},{9,10},{11,12},{13,14},{15,16},{17,18},{19... | collective-permute-start | bytes 663560 | tf_op jit(solution)/shard_map/ppermute | solution.py:559
  20.6 1.2 %begin.1 = (f32[16,64,256]{2,1,0:T(8,128)S(1)}, f32[16,64,512]{2,1,0:T(8,128)S(1)}) custom-call(f32[64,16,256]{2,1,0:T(8,128)S(1)} %get-tuple-element.18.vec_ref, bf16[256,512]{1,0:T(8,128)(2,1)S(1)} %get-tuple-element.17.table_ref.refs_4_), custom_call_target="tpu_custom_call" | custom-call | flops 805306368 | tf_op jit(solution)/shard_map/begin/pallas_call | solution.py:191
  21.8 0.0 collective-permute-done.refs_2_
  21.8 4.1 %collective-permute-done.1.refs_3_ = f32[3,72,256]{2,1,0:T(8,128)S(1)} collective-permute-done((f32[3,72,256]{2,1,0:T(8,128)S(1)}, f32[3,72,256]{2,1,0:T(8,128)S(1)}, u32[]{:S(2)}, u32[]{:S(2)}) %collective-permute-start.1) | collective-permute-done | bytes 221216 | tf_op jit(solution)/shard_map/ppermute | solution.py:559
  25.9 6.0 %operator_gram.1 = (f32[16,64,256]{2,1,0:T(8,128)S(1)}, f32[64,1,128]{2,1,0:T(1,128)S(1)}) custom-call(s32[3]{0:T(128)S(1)} %pad_add_fusion.odd_ref.refs_0_, f32[16,256]{1,0:T(8,128)S(1)} %get-tuple-element.14.refs_1_, f32[3,72,256]{2,1,0:T(8,128)S(1)} %collective-permute-done.refs_2_, f32[3,72,256]{2,1,0:T(8,128)S(1)} %collective-permute-done.1.refs_3_, ...), custom_call_target="tpu_custom_call" | custom-call | flops 2214592512 | tf_op jit(solution)/shard_map/operator_gram/pallas_call | solution.py:323
  31.9 11.5 %all_to_all.15.parts_ref = f32[64,1,128]{2,1,0:T(1,128)S(1)} all-to-all(f32[64,1,128]{2,1,0:T(1,128)S(1)} %get-tuple-element.22), channel_id=1, replica_groups=mesh['sfc_0'=16,'sfc_1'=8,'sub_0'=4,'sub_1'=2] {'sfc_1','sub_0','sub_1'}, dimensions={0} | all-to-all | bytes 65536 | tf_op jit(solution)/shard_map/all_to_all | solution.py:369
  43.4 0.2 pair_sum.2
  43.6 27.8 %all_to_all.16.parts_ref = f32[16,1,128]{2,1,0:T(1,128)S(1)} all-to-all(f32[16,1,128]{2,1,0:T(1,128)S(1)} %pair_sum.2), channel_id=1, replica_groups=mesh['sfc_0'=16,'sfc_1'=8,'sub_0'=4,'sub_1'=2] {'sfc_0'}, dimensions={0} | all-to-all | bytes 16384 | tf_op jit(solution)/shard_map/all_to_all | solution.py:371
  71.4 0.2 pair_sum.3
  71.6 14.8 %all_to_all.17.refs_0_ = f32[64,1,128]{2,1,0:T(1,128)S(1)} all-to-all(f32[64,1,128]{2,1,0:T(1,128)S(1)} %pair_sum.3), channel_id=1, replica_groups=mesh['sfc_0'=16,'sfc_1'=8,'sub_0'=4,'sub_1'=2] {'sfc_1','sub_0','sub_1'}, dimensions={0} | all-to-all | bytes 65536 | tf_op jit(solution)/shard_map/all_to_all | solution.py:372
  86.4 5.7 %factor.1 = (f32[64,64]{1,0:T(8,128)S(1)}, f32[64,64]{1,0:T(8,128)S(1)}, f32[64,64]{1,0:T(8,128)}) custom-call(f32[64,1,128]{2,1,0:T(1,128)S(1)} %all_to_all.17.refs_0_), custom_call_target="tpu_custom_call" | custom-call | tf_op jit(solution)/shard_map/factor/pallas_call | solution.py:509
  92.1 1.7 %basis.1 = f32[64,16,256]{2,1,0:T(8,128)} custom-call(f32[16,64,256]{2,1,0:T(8,128)S(1)} %get-tuple-element.21.w_ref, f32[64,64]{1,0:T(8,128)S(1)} %get-tuple-element.23.high_ref, f32[64,64]{1,0:T(8,128)S(1)} %get-tuple-element.24.low_ref), custom_call_target="tpu_custom_call" | custom-call | tf_op jit(solution)/shard_map/basis/pallas_call | solution.py:540
Async XLA Ops:
  2.6 19.2 %collective-permute-start = (f32[3,72,256]{2,1,0:T(8,128)S(1)}, f32[3,72,256]{2,1,0:T(8,128)S(1)}, u32[]{:S(2)}, u32[]{:S(2)}) collective-permute-start(f32[3,72,256]{2,1,0:T(8,128)S(1)} %get-tuple-element.15), channel_id=1, source_target_pairs={{0,1},{2,3},{4,5},{6,7},{8,9},{10,11},{12,13},{14,15},{16,17},{18,... | collective-permute-start | bytes 663560 | tf_op jit(solution)/shard_map/ppermute | solution.py:560
  18.6 7.3 %collective-permute-start.1 = (f32[3,72,256]{2,1,0:T(8,128)S(1)}, f32[3,72,256]{2,1,0:T(8,128)S(1)}, u32[]{:S(2)}, u32[]{:S(2)}) collective-permute-start(f32[3,72,256]{2,1,0:T(8,128)S(1)} %get-tuple-element.16), channel_id=1, source_target_pairs={{1,2},{3,4},{5,6},{7,8},{9,10},{11,12},{13,14},{15,16},{17,18},{19... | collective-permute-start | bytes 663560 | tf_op jit(solution)/shard_map/ppermute | solution.py:559

commit v5 on v4

--- a/solution.py
+++ b/solution.py
@@ -173,45 +173,69 @@
     both[pl.ds(start, count)] = (parts[:n] + parts[n : 2 * n] + parts[2 * n :]).reshape(count, k, 2 * PLANE)
 
 
-def begin_kernel(vec_ref, table_ref, field, both):
+def begin_kernel(vec_ref, react_ref, table_ref, own, own_both, first, first_both):
     _, nx, _ = vec_ref.shape
     for x in range(nx):
-        field[x] = vec_ref[:, x, :]
+        own[x] = vec_ref[:, x, :]
     table = table_ref[...]
 
-    def one_part(i, _):
-        products(field, both, table, 0, nx)
-        return 0
-
-    lax.fori_loop(0, 1, one_part, 0)
-
-
-def begin(vectors, table):
+    def own_products(i, _):
+        products(own, own_both, table, 0, nx)
+        return 0
+
+    lax.fori_loop(0, 1, own_products, 0)
+
+    def inside(x, _):
+        first[x - 1] = combination(own_both, own, react_ref, x, x)
+        return 0
+
+    lax.fori_loop(1, nx - 1, inside, 0, unroll=7)
+
+    def first_products(i, _):
+        products(first, first_both, table, 0, nx - 2)
+        return 0
+
+    lax.fori_loop(0, 1, first_products, 0)
+
+
+def combination(both, field, react, x, at):
+    return (both[x - 1, :, :PLANE] + both[x + 1, :, :PLANE] + both[x, :, PLANE:]) * (1.0 / 216.0) + react[
+        pl.ds(at, 1), :
+    ] * field[x]
+
+
+def begin(vectors, reaction, table):
     k, nx, plane = vectors.shape
     return pl.pallas_call(
         begin_kernel,
-        out_shape=(in_vmem(nx, k, plane), in_vmem(nx, k, 2 * plane)),
-        in_specs=[VMEM_SPEC, VMEM_SPEC],
-        out_specs=(VMEM_SPEC, VMEM_SPEC),
-        cost_estimate=pl.CostEstimate(flops=2 * 3 * nx * k * plane * 2 * plane, bytes_accessed=0, transcendentals=0),
+        out_shape=(
+            in_vmem(nx, k, plane),
+            in_vmem(nx, k, 2 * plane),
+            in_vmem(nx - 2, k, plane),
+            in_vmem(nx - 2, k, 2 * plane),
+        ),
+        in_specs=[VMEM_SPEC] * 3,
+        out_specs=(VMEM_SPEC,) * 4,
+        cost_estimate=pl.CostEstimate(flops=12 * (nx + nx - 2) * k * plane * plane, bytes_accessed=0, transcendentals=0),
         compiler_params=SMALL,
         name="begin",
-    )(vmem(vectors), vmem(table))
-
-
-def operator_kernel(k, nx, flags_ref, react_ref, inner_ref, outer_ref, table_ref, own_ref, own_both_ref, w_ref, gram_ref, field, both, react):
+    )(vmem(vectors), vmem(reaction), vmem(table))
+
+
+def operator_kernel(k, nx, flags_ref, react_ref, inner_ref, outer_ref, table_ref, own, own_both, first, first_both, w_ref, gram_ref, field, both, react):
     halo = POWERS
     total = nx + 2 * halo
+    top = halo + nx
     odd = flags_ref[0]
     low_inside = flags_ref[1].astype(F32)
     high_inside = flags_ref[2].astype(F32)
-    react[halo : halo + nx] = react_ref[...]
+    react[halo:top] = react_ref[...]
 
     def fill(low_ref, high_ref):
         field[0:halo] = low_ref[:, :k, :]
-        field[halo + nx : total] = high_ref[:, :k, :]
+        field[top:total] = high_ref[:, :k, :]
         react[0:halo] = low_ref[:, k, :]
-        react[halo + nx : total] = high_ref[:, k, :]
+        react[top:total] = high_ref[:, k, :]
 
     @pl.when(odd == 0)
     def _():
@@ -223,54 +247,61 @@
 
     table = table_ref[...]
 
-    def combine(step, x, values, parts, offset):
-        value = (
-            parts[x - 1 - offset, :, :PLANE] + parts[x + 1 - offset, :, :PLANE] + parts[x - offset, :, PLANE:]
-        ) * (1.0 / 216.0) + react[pl.ds(x, 1), :] * values[x - offset]
-        if step < POWERS - 1:
-            keep = jnp.where(x < halo, low_inside, jnp.where(x >= halo + nx, high_inside, 1.0))
-            field[x] = value * keep
-        else:
-            w_ref[x - halo] = value
-        return 0
-
-    def edge(i, _):
-        products(field, both, table, i * (halo + nx), halo)
-        return 0
-
-    lax.fori_loop(0, 2, edge, 0)
-
-    def own_edge(i, _):
-        x = jnp.where(i < 2, i, nx - 4 + i)
-        field[halo + x] = own_ref[x]
-        both[halo + x] = own_both_ref[x]
-        return 0
-
-    lax.fori_loop(0, 4, own_edge, 0)
-
-    def outside(i, _):
-        x = jnp.where(i < halo, 1 + i, nx - 1 + i)
-        return combine(0, x, field, both, 0)
-
-    lax.fori_loop(0, 2 * halo, outside, 0)
+    def keep(x):
+        return jnp.where(x < halo, low_inside, jnp.where(x >= top, high_inside, 1.0))
+
+    def step(x, _):
+        field[x] = combination(both, field, react, x, x) * keep(x)
+        return 0
+
+    def ends(body, low, high, count):
+        lax.fori_loop(0, 2 * count, lambda i, c: body(jnp.where(i < count, low + i, high + i - count), c), 0, unroll=count)
+
+    def border_products(i, _):
+        products(field, both, table, i * top, halo)
+        return 0
+
+    lax.fori_loop(0, 2, border_products, 0)
+
+    def own_edge(x, _):
+        field[x] = own[x - halo]
+        both[x] = own_both[x - halo]
+        return 0
+
+    ends(own_edge, halo, top - 2, 2)
+    ends(step, 1, top - 1, 3)
+
+    def edge_products(i, _):
+        products(field, both, table, 1 + i * (top - 2), halo)
+        return 0
+
+    lax.fori_loop(0, 2, edge_products, 0)
+
+    def first_edge(x, _):
+        field[x] = first[x - halo - 1]
+        both[x] = first_both[x - halo - 1]
+        return 0
+
+    ends(first_edge, halo + 1, top - 3, 2)
+    ends(step, 2, top - 2, 3)
 
     def inside(x, _):
-        return combine(0, x, own_ref, own_both_ref, halo)
-
-    lax.fori_loop(halo + 1, halo + nx - 1, inside, 0, unroll=7)
-    for step in range(1, POWERS):
-        first, last = step, total - step
-
-        def product(i, _):
-            products(field, both, table, first, last - first)
-            return 0
-
-        lax.fori_loop(0, 1, product, 0)
-
-        def later(x, _):
-            return combine(step, x, field, both, 0)
-
-        lax.fori_loop(first + 1, last - 1, later, 0, unroll=(last - first - 2) // 2)
+        field[x] = combination(first_both, first, react, x - halo - 1, x)
+        return 0
+
+    lax.fori_loop(halo + 2, top - 2, inside, 0, unroll=6)
+
+    def third_products(i, _):
+        products(field, both, table, 2, total - 4)
+        return 0
+
+    lax.fori_loop(0, 1, third_products, 0)
+
+    def last(x, _):
+        w_ref[x - halo] = combination(both, field, react, x, x)
+        return 0
+
+    lax.fori_loop(halo, top, last, 0, unroll=8)
     peak = jnp.abs(w_ref[0])
     for x in range(1, nx):
         peak = jnp.maximum(peak, jnp.abs(w_ref[x]))
@@ -316,24 +347,24 @@
     gram_ref[:, 0, :] = jnp.concatenate([high * row * column, err * row * column], axis=1)
 
 
-def operator_and_gram(flags, reaction, inner, outer, table, own, own_both):
-    nx, k, plane = own.shape
+def operator_and_gram(flags, reaction, inner, outer, table, begun):
+    nx, k, plane = begun[0].shape
     total = nx + 2 * POWERS
     smem = pl.BlockSpec(memory_space=pltpu.SMEM)
     return pl.pallas_call(
         lambda *refs: operator_kernel(k, nx, *refs),
         out_shape=(in_vmem(nx, k, plane), in_vmem(k, 1, 2 * k)),
-        in_specs=[smem] + [VMEM_SPEC] * 6,
+        in_specs=[smem] + [VMEM_SPEC] * 8,
         out_specs=(VMEM_SPEC, VMEM_SPEC),
         scratch_shapes=[
             pltpu.VMEM((total, k, plane), F32),
             pltpu.VMEM((total, k, 2 * plane), F32),
-            pltpu.VMEM((total, plane), F32),
+            pltpu.VMEM((total + 18, plane), F32),
         ],
-        cost_estimate=pl.CostEstimate(flops=2 * 3 * 44 * k * plane * 2 * plane, bytes_accessed=0, transcendentals=0),
+        cost_estimate=pl.CostEstimate(flops=2 * 3 * 30 * k * plane * 2 * plane, bytes_accessed=0, transcendentals=0),
         compiler_params=SMALL,
         name="operator_gram",
-    )(flags, vmem(reaction), vmem(inner), vmem(outer), vmem(table), vmem(own), vmem(own_both))
+    )(flags, vmem(reaction), vmem(inner), vmem(outer), vmem(table), *map(vmem, begun))
 
 
 def pair_sum_kernel(parts_ref, out_ref):
@@ -474,12 +505,12 @@
     counts = dot(guess_stack, jnp.concatenate(gram_digits, axis=1))
     high, low = levels_to_pair(level_sums(counts, k, 3, 6))
     product = (high + low) * (top * 2.0**-11)
-    big, big_inverse = power_below(jnp.max(jnp.abs(high), axis=1, keepdims=True))
-    product_digits = digits(high * big_inverse * 64.0, 6, extra=low * big_inverse * 64.0)
+    to_digits = top * 2.0**-6
+    product_digits = digits(high * to_digits, 6, extra=low * to_digits)
     counts = dot_t(jnp.concatenate(product_digits, axis=0), guess_stack)
     high, low = levels_to_pair(level_sums(counts, k, 6, 3))
     top_row = jnp.sum(jnp.where(eye, top, 0.0), axis=0, keepdims=True)
-    unit = (top * 2.0**-11) * (big * (1.0 / 64.0)) * (top_row * (1.0 / 64.0))
+    unit = 2.0**-11 * top_row
     high = high * unit
     low = low * unit
     delta = jnp.where(eye, high - 1.0, high) + low
@@ -558,8 +589,8 @@
     within = [(i, i + 1) for i in range(0, peers, 2)]
     outer = lax.ppermute(outer, SFC_SUB, across + [(b, a) for a, b in across])
     inner = lax.ppermute(inner, SFC_SUB, within + [(b, a) for a, b in within])
-    field, both = begin(vectors, table)
-    w, gram = operator_and_gram(flags, reaction, inner, outer, table, field, both)
+    begun = begin(vectors, reaction, table)
+    w, gram = operator_and_gram(flags, reaction, inner, outer, table, begun)
     gram = sum_over_devices(gram)
     high, low, upper = factor(gram, math.sqrt(peers * nx * plane))
     return basis_of(w, high, low), upper

time: 94.1 us -> 93.4 us (level)
  waiting for transfers between devices: 4.1 us -> 2.97 us
    ppermute x1, waiting for transfers between devices: 4.1 us -> 2.96 us  [device_program(): outer = lax.ppermute(outer, SFC_SUB, across + [(b, a) for a, b in across])]
    pallas_call x1, Pallas kernels: 1.21 us -> 2.35 us  [begin(): pl.pallas_call(begin_kernel, out_shape=(in_vmem(nx, k, plane), in_vmem(nx...]
  transfers between devices with their start and end apart: 2 -> 2, of which waited for: 1 -> 1; matrix products, arithmetic and copies ran while one was open for 0% -> 0% of each run, Pallas kernels for 1% -> 3%
where the time goes in v5:
time: 93.4 us; the launch traced here: 93.1 us
  blocking collectives  54.2 us (58%)
  starting transfers between devices  17.9 us (19%)
  Pallas kernels  17.3 us (19%)
  waiting for transfers between devices  2.97 us (3%)
    all_to_all x1, blocking collectives, sum_over_devices(): mine = pair_sum(lax.all_to_all(mine, FAR, 0, 0), near)  27.8 us
    ppermute x1, starting transfers between devices, device_program(): inner = lax.ppermute(inner, SFC_SUB, within + [(b, a) for a, b in within])  16 us
    all_to_all x1, blocking collectives, sum_over_devices(): return lax.all_to_all(mine, NEAR, 0, 0)  14.8 us
    all_to_all x1, blocking collectives, sum_over_devices(): rows = lax.all_to_all(gram, NEAR, 0, 0)  11.5 us
    pallas_call x1, Pallas kernels, factor(): pl.pallas_call(lambda *refs: factor_kernel(scale, *refs), out_shape=(in_v...  5.63 us
    pallas_call x1, Pallas kernels, operator_and_gram(): pl.pallas_call(lambda *refs: operator_kernel(k, nx, *refs), out_shape=(in...  5.32 us
    ppermute x1, waiting for transfers between devices, device_program(): outer = lax.ppermute(outer, SFC_SUB, across + [(b, a) for a, b in across])  2.96 us
    pallas_call x1, Pallas kernels, begin(): pl.pallas_call(begin_kernel, out_shape=(in_vmem(nx, k, plane), in_vmem(nx...  2.35 us
  transfers between devices with their start and end apart: 2, of which 1 were waited for; matrix products, arithmetic and copies ran while one was open for 0% of the time, Pallas kernels for 3%

profile of v5, /device:TPU:1, one launch (start us, length us, event | category | flops | bytes accessed | tf_op | source)
XLA Modules:
  0.0 93.1 jit_solution(11244285036676334909)
XLA Ops:
  0.6 0.1 pad_add_fusion.odd_ref.refs_0_
  0.7 1.9 %borders.1 = (f32[3,72,256]{2,1,0:T(8,128)S(1)}, f32[3,72,256]{2,1,0:T(8,128)S(1)}, f32[64,16,256]{2,1,0:T(8,128)S(1)}, f32[16,256]{1,0:T(8,128)S(1)}, bf16[256,512]{1,0:T(8,128)(2,1)S(1)}) custom-call(s32[3]{0:T(128)S(1)} %pad_add_fusion.odd_ref.refs_0_, f32[64,16,256]{2,1,0:T(8,128)} %vec_ref.1, f32[16,256]{1,0:T(8,128)} %react_ref.1, ...), custom_call_target="tpu_custom_call" | custom-call | tf_op jit(solution)/shard_map/borders/pallas_call | solution.py:157
  2.6 16.0 %collective-permute-start = (f32[3,72,256]{2,1,0:T(8,128)S(1)}, f32[3,72,256]{2,1,0:T(8,128)S(1)}, u32[]{:S(2)}, u32[]{:S(2)}) collective-permute-start(f32[3,72,256]{2,1,0:T(8,128)S(1)} %get-tuple-element.17), channel_id=1, source_target_pairs={{0,1},{2,3},{4,5},{6,7},{8,9},{10,11},{12,13},{14,15},{16,17},{18,... | collective-permute-start | bytes 663560 | tf_op jit(solution)/shard_map/ppermute | solution.py:591
  18.6 1.9 %collective-permute-start.1 = (f32[3,72,256]{2,1,0:T(8,128)S(1)}, f32[3,72,256]{2,1,0:T(8,128)S(1)}, u32[]{:S(2)}, u32[]{:S(2)}) collective-permute-start(f32[3,72,256]{2,1,0:T(8,128)S(1)} %get-tuple-element.18), channel_id=1, source_target_pairs={{1,2},{3,4},{5,6},{7,8},{9,10},{11,12},{13,14},{15,16},{17,18},{19... | collective-permute-start | bytes 663560 | tf_op jit(solution)/shard_map/ppermute | solution.py:590
  20.6 2.3 %begin.1 = (f32[16,64,256]{2,1,0:T(8,128)S(1)}, f32[16,64,512]{2,1,0:T(8,128)S(1)}, f32[14,64,256]{2,1,0:T(8,128)S(1)}, f32[14,64,512]{2,1,0:T(8,128)S(1)}) custom-call(f32[64,16,256]{2,1,0:T(8,128)S(1)} %get-tuple-element.20.vec_ref, f32[16,256]{1,0:T(8,128)S(1)} %get-tuple-element.16.react_ref.refs_1_, bf16[256,512]{1,0:T(8,128)(2,1)S(1)} %get-tuple-element.19.table_ref.refs_4_), custom_call_target="tpu_custom_call" | custom-call | flops 1509949440 | tf_op jit(solution)/shard_map/begin/pallas_call | solution.py:209
  22.9 0.0 collective-permute-done.refs_2_
  22.9 3.0 %collective-permute-done.1.refs_3_ = f32[3,72,256]{2,1,0:T(8,128)S(1)} collective-permute-done((f32[3,72,256]{2,1,0:T(8,128)S(1)}, f32[3,72,256]{2,1,0:T(8,128)S(1)}, u32[]{:S(2)}, u32[]{:S(2)}) %collective-permute-start.1) | collective-permute-done | bytes 221216 | tf_op jit(solution)/shard_map/ppermute | solution.py:590
  25.9 5.3 %operator_gram.1 = (f32[16,64,256]{2,1,0:T(8,128)S(1)}, f32[64,1,128]{2,1,0:T(1,128)S(1)}) custom-call(s32[3]{0:T(128)S(1)} %pad_add_fusion.odd_ref.refs_0_, f32[16,256]{1,0:T(8,128)S(1)} %get-tuple-element.16.react_ref.refs_1_, f32[3,72,256]{2,1,0:T(8,128)S(1)} %collective-permute-done.refs_2_, f32[3,72,256]{2,1,0:T(8,128)S(1)} %collective-permute-done.1.refs_3_, ...), custom_call_target="tpu_custom_call" | custom-call | flops 1509949440 | tf_op jit(solution)/shard_map/operator_gram/pallas_call | solution.py:354
  31.2 11.5 %all_to_all.15.parts_ref = f32[64,1,128]{2,1,0:T(1,128)S(1)} all-to-all(f32[64,1,128]{2,1,0:T(1,128)S(1)} %get-tuple-element.26), channel_id=1, replica_groups=mesh['sfc_0'=16,'sfc_1'=8,'sub_0'=4,'sub_1'=2] {'sfc_1','sub_0','sub_1'}, dimensions={0} | all-to-all | bytes 65536 | tf_op jit(solution)/shard_map/all_to_all | solution.py:400
  42.8 0.2 pair_sum.2
  43.0 27.8 %all_to_all.16.parts_ref = f32[16,1,128]{2,1,0:T(1,128)S(1)} all-to-all(f32[16,1,128]{2,1,0:T(1,128)S(1)} %pair_sum.2), channel_id=1, replica_groups=mesh['sfc_0'=16,'sfc_1'=8,'sub_0'=4,'sub_1'=2] {'sfc_0'}, dimensions={0} | all-to-all | bytes 16384 | tf_op jit(solution)/shard_map/all_to_all | solution.py:402
  70.8 0.2 pair_sum.3
  70.9 14.8 %all_to_all.17.refs_0_ = f32[64,1,128]{2,1,0:T(1,128)S(1)} all-to-all(f32[64,1,128]{2,1,0:T(1,128)S(1)} %pair_sum.3), channel_id=1, replica_groups=mesh['sfc_0'=16,'sfc_1'=8,'sub_0'=4,'sub_1'=2] {'sfc_1','sub_0','sub_1'}, dimensions={0} | all-to-all | bytes 65536 | tf_op jit(solution)/shard_map/all_to_all | solution.py:403
  85.8 5.6 %factor.1 = (f32[64,64]{1,0:T(8,128)S(1)}, f32[64,64]{1,0:T(8,128)S(1)}, f32[64,64]{1,0:T(8,128)}) custom-call(f32[64,1,128]{2,1,0:T(1,128)S(1)} %all_to_all.17.refs_0_), custom_call_target="tpu_custom_call" | custom-call | tf_op jit(solution)/shard_map/factor/pallas_call | solution.py:540
  91.4 1.7 %basis.1 = f32[64,16,256]{2,1,0:T(8,128)} custom-call(f32[16,64,256]{2,1,0:T(8,128)S(1)} %get-tuple-element.25.w_ref, f32[64,64]{1,0:T(8,128)S(1)} %get-tuple-element.27.high_ref, f32[64,64]{1,0:T(8,128)S(1)} %get-tuple-element.28.low_ref), custom_call_target="tpu_custom_call" | custom-call | tf_op jit(solution)/shard_map/basis/pallas_call | solution.py:571
Async XLA Ops:
  2.6 20.3 %collective-permute-start = (f32[3,72,256]{2,1,0:T(8,128)S(1)}, f32[3,72,256]{2,1,0:T(8,128)S(1)}, u32[]{:S(2)}, u32[]{:S(2)}) collective-permute-start(f32[3,72,256]{2,1,0:T(8,128)S(1)} %get-tuple-element.17), channel_id=1, source_target_pairs={{0,1},{2,3},{4,5},{6,7},{8,9},{10,11},{12,13},{14,15},{16,17},{18,... | collective-permute-start | bytes 663560 | tf_op jit(solution)/shard_map/ppermute | solution.py:591
  18.6 7.3 %collective-permute-start.1 = (f32[3,72,256]{2,1,0:T(8,128)S(1)}, f32[3,72,256]{2,1,0:T(8,128)S(1)}, u32[]{:S(2)}, u32[]{:S(2)}) collective-permute-start(f32[3,72,256]{2,1,0:T(8,128)S(1)} %get-tuple-element.18), channel_id=1, source_target_pairs={{1,2},{3,4},{5,6},{7,8},{9,10},{11,12},{13,14},{15,16},{17,18},{19... | collective-permute-start | bytes 663560 | tf_op jit(solution)/shard_map/ppermute | solution.py:590

commit v6 on v5

--- a/solution.py
+++ b/solution.py
@@ -549,15 +549,21 @@
 
 
 def basis_kernel(w_ref, high_ref, low_ref, out_ref, result, sems):
-    _, nx, _ = result.shape
+    k, nx, _ = result.shape
     p1, p2, p3 = split3(high_ref[...])
     p4 = low_ref[...].astype(BF16)
-    left = jnp.concatenate([p1, p1, p1, p2, p2, p3, p4], axis=1)
+    left = jnp.concatenate(
+        [
+            jnp.concatenate([p1, p1, p1, p2], axis=1),
+            jnp.concatenate([jnp.zeros_like(p1), p2, p4, p3], axis=1),
+        ],
+        axis=0,
+    )
     copies = []
     for x in range(nx):
         w1, w2, w3 = split3(w_ref[x])
-        right = jnp.concatenate([w3, w2, w1, w2, w1, w1, w1], axis=0)
-        result[:, x, :] = dot(left, right)
+        both = dot(left, jnp.concatenate([w3, w2, w1, w1], axis=0))
+        result[:, x, :] = both[:k] + both[k:]
         if (x + 1) % 8 == 0:
             rows = pl.ds(x - 7, 8)
             copies.append(pltpu.make_async_copy(result.at[:, rows, :], out_ref.at[:, rows, :], sems.at[x // 8]))

time: 93.4 us -> 93.2 us (level)
  no operation moved by 1% of the time
where the time goes in v6:
time: 93.2 us; the launch traced here: 92.9 us
  blocking collectives  54.2 us (58%)
  starting transfers between devices  17.9 us (19%)
  Pallas kernels  17 us (18%)
  waiting for transfers between devices  2.97 us (3%)
    all_to_all x1, blocking collectives, sum_over_devices(): mine = pair_sum(lax.all_to_all(mine, FAR, 0, 0), near)  27.8 us
    ppermute x1, starting transfers between devices, device_program(): inner = lax.ppermute(inner, SFC_SUB, within + [(b, a) for a, b in within])  16 us
    all_to_all x1, blocking collectives, sum_over_devices(): return lax.all_to_all(mine, NEAR, 0, 0)  14.8 us
    all_to_all x1, blocking collectives, sum_over_devices(): rows = lax.all_to_all(gram, NEAR, 0, 0)  11.5 us
    pallas_call x1, Pallas kernels, factor(): pl.pallas_call(lambda *refs: factor_kernel(scale, *refs), out_shape=(in_v...  5.63 us
    pallas_call x1, Pallas kernels, operator_and_gram(): pl.pallas_call(lambda *refs: operator_kernel(k, nx, *refs), out_shape=(in...  5.32 us
    ppermute x1, waiting for transfers between devices, device_program(): outer = lax.ppermute(outer, SFC_SUB, across + [(b, a) for a, b in across])  2.96 us
    pallas_call x1, Pallas kernels, begin(): pl.pallas_call(begin_kernel, out_shape=(in_vmem(nx, k, plane), in_vmem(nx...  2.35 us
  transfers between devices with their start and end apart: 2, of which 1 were waited for; matrix products, arithmetic and copies ran while one was open for 0% of the time, Pallas kernels for 3%

profile of v6, /device:TPU:1, one launch (start us, length us, event | category | flops | bytes accessed | tf_op | source)
XLA Modules:
  0.0 92.9 jit_solution(4880596938432252225)
XLA Ops:
  0.6 0.1 pad_add_fusion.odd_ref.refs_0_
  0.7 1.9 %borders.1 = (f32[3,72,256]{2,1,0:T(8,128)S(1)}, f32[3,72,256]{2,1,0:T(8,128)S(1)}, f32[64,16,256]{2,1,0:T(8,128)S(1)}, f32[16,256]{1,0:T(8,128)S(1)}, bf16[256,512]{1,0:T(8,128)(2,1)S(1)}) custom-call(s32[3]{0:T(128)S(1)} %pad_add_fusion.odd_ref.refs_0_, f32[64,16,256]{2,1,0:T(8,128)} %vec_ref.1, f32[16,256]{1,0:T(8,128)} %react_ref.1, ...), custom_call_target="tpu_custom_call" | custom-call | tf_op jit(solution)/shard_map/borders/pallas_call | solution.py:157
  2.6 16.0 %collective-permute-start = (f32[3,72,256]{2,1,0:T(8,128)S(1)}, f32[3,72,256]{2,1,0:T(8,128)S(1)}, u32[]{:S(2)}, u32[]{:S(2)}) collective-permute-start(f32[3,72,256]{2,1,0:T(8,128)S(1)} %get-tuple-element.17), channel_id=1, source_target_pairs={{0,1},{2,3},{4,5},{6,7},{8,9},{10,11},{12,13},{14,15},{16,17},{18,... | collective-permute-start | bytes 663560 | tf_op jit(solution)/shard_map/ppermute | solution.py:597
  18.6 1.9 %collective-permute-start.1 = (f32[3,72,256]{2,1,0:T(8,128)S(1)}, f32[3,72,256]{2,1,0:T(8,128)S(1)}, u32[]{:S(2)}, u32[]{:S(2)}) collective-permute-start(f32[3,72,256]{2,1,0:T(8,128)S(1)} %get-tuple-element.18), channel_id=1, source_target_pairs={{1,2},{3,4},{5,6},{7,8},{9,10},{11,12},{13,14},{15,16},{17,18},{19... | collective-permute-start | bytes 663560 | tf_op jit(solution)/shard_map/ppermute | solution.py:596
  20.6 2.3 %begin.1 = (f32[16,64,256]{2,1,0:T(8,128)S(1)}, f32[16,64,512]{2,1,0:T(8,128)S(1)}, f32[14,64,256]{2,1,0:T(8,128)S(1)}, f32[14,64,512]{2,1,0:T(8,128)S(1)}) custom-call(f32[64,16,256]{2,1,0:T(8,128)S(1)} %get-tuple-element.20.vec_ref, f32[16,256]{1,0:T(8,128)S(1)} %get-tuple-element.16.react_ref.refs_1_, bf16[256,512]{1,0:T(8,128)(2,1)S(1)} %get-tuple-element.19.table_ref.refs_4_), custom_call_target="tpu_custom_call" | custom-call | flops 1509949440 | tf_op jit(solution)/shard_map/begin/pallas_call | solution.py:209
  22.9 0.0 collective-permute-done.refs_2_
  22.9 3.0 %collective-permute-done.1.refs_3_ = f32[3,72,256]{2,1,0:T(8,128)S(1)} collective-permute-done((f32[3,72,256]{2,1,0:T(8,128)S(1)}, f32[3,72,256]{2,1,0:T(8,128)S(1)}, u32[]{:S(2)}, u32[]{:S(2)}) %collective-permute-start.1) | collective-permute-done | bytes 221216 | tf_op jit(solution)/shard_map/ppermute | solution.py:596
  25.9 5.3 %operator_gram.1 = (f32[16,64,256]{2,1,0:T(8,128)S(1)}, f32[64,1,128]{2,1,0:T(1,128)S(1)}) custom-call(s32[3]{0:T(128)S(1)} %pad_add_fusion.odd_ref.refs_0_, f32[16,256]{1,0:T(8,128)S(1)} %get-tuple-element.16.react_ref.refs_1_, f32[3,72,256]{2,1,0:T(8,128)S(1)} %collective-permute-done.refs_2_, f32[3,72,256]{2,1,0:T(8,128)S(1)} %collective-permute-done.1.refs_3_, ...), custom_call_target="tpu_custom_call" | custom-call | flops 1509949440 | tf_op jit(solution)/shard_map/operator_gram/pallas_call | solution.py:354
  31.2 11.5 %all_to_all.15.parts_ref = f32[64,1,128]{2,1,0:T(1,128)S(1)} all-to-all(f32[64,1,128]{2,1,0:T(1,128)S(1)} %get-tuple-element.26), channel_id=1, replica_groups=mesh['sfc_0'=16,'sfc_1'=8,'sub_0'=4,'sub_1'=2] {'sfc_1','sub_0','sub_1'}, dimensions={0} | all-to-all | bytes 65536 | tf_op jit(solution)/shard_map/all_to_all | solution.py:400
  42.8 0.2 pair_sum.2
  43.0 27.8 %all_to_all.16.parts_ref = f32[16,1,128]{2,1,0:T(1,128)S(1)} all-to-all(f32[16,1,128]{2,1,0:T(1,128)S(1)} %pair_sum.2), channel_id=1, replica_groups=mesh['sfc_0'=16,'sfc_1'=8,'sub_0'=4,'sub_1'=2] {'sfc_0'}, dimensions={0} | all-to-all | bytes 16384 | tf_op jit(solution)/shard_map/all_to_all | solution.py:402
  70.8 0.2 pair_sum.3
  70.9 14.8 %all_to_all.17.refs_0_ = f32[64,1,128]{2,1,0:T(1,128)S(1)} all-to-all(f32[64,1,128]{2,1,0:T(1,128)S(1)} %pair_sum.3), channel_id=1, replica_groups=mesh['sfc_0'=16,'sfc_1'=8,'sub_0'=4,'sub_1'=2] {'sfc_1','sub_0','sub_1'}, dimensions={0} | all-to-all | bytes 65536 | tf_op jit(solution)/shard_map/all_to_all | solution.py:403
  85.8 5.6 %factor.1 = (f32[64,64]{1,0:T(8,128)S(1)}, f32[64,64]{1,0:T(8,128)S(1)}, f32[64,64]{1,0:T(8,128)}) custom-call(f32[64,1,128]{2,1,0:T(1,128)S(1)} %all_to_all.17.refs_0_), custom_call_target="tpu_custom_call" | custom-call | tf_op jit(solution)/shard_map/factor/pallas_call | solution.py:540
  91.4 1.5 %basis.1 = f32[64,16,256]{2,1,0:T(8,128)} custom-call(f32[16,64,256]{2,1,0:T(8,128)S(1)} %get-tuple-element.25.w_ref, f32[64,64]{1,0:T(8,128)S(1)} %get-tuple-element.27.high_ref, f32[64,64]{1,0:T(8,128)S(1)} %get-tuple-element.28.low_ref), custom_call_target="tpu_custom_call" | custom-call | tf_op jit(solution)/shard_map/basis/pallas_call | solution.py:577
Async XLA Ops:
  2.6 20.3 %collective-permute-start = (f32[3,72,256]{2,1,0:T(8,128)S(1)}, f32[3,72,256]{2,1,0:T(8,128)S(1)}, u32[]{:S(2)}, u32[]{:S(2)}) collective-permute-start(f32[3,72,256]{2,1,0:T(8,128)S(1)} %get-tuple-element.17), channel_id=1, source_target_pairs={{0,1},{2,3},{4,5},{6,7},{8,9},{10,11},{12,13},{14,15},{16,17},{18,... | collective-permute-start | bytes 663560 | tf_op jit(solution)/shard_map/ppermute | solution.py:597
  18.6 7.3 %collective-permute-start.1 = (f32[3,72,256]{2,1,0:T(8,128)S(1)}, f32[3,72,256]{2,1,0:T(8,128)S(1)}, u32[]{:S(2)}, u32[]{:S(2)}) collective-permute-start(f32[3,72,256]{2,1,0:T(8,128)S(1)} %get-tuple-element.18), channel_id=1, source_target_pairs={{1,2},{3,4},{5,6},{7,8},{9,10},{11,12},{13,14},{15,16},{17,18},{19... | collective-permute-start | bytes 663560 | tf_op jit(solution)/shard_map/ppermute | solution.py:596
